TPU v7x, 128 devices: a whole 4x4x4 slice. The times are simulated.
128 devices in a mesh: seq: 16 (over x, y), head: 8 (over z, core).
Axes of the slice: x: 4, y: 4, z: 4, core: 2. Of those that a mesh axis runs over, the one named last changes fastest.
Arguments:
- queries: bfloat16 [4096, 12288], P('seq', 'head'), may hold values from -256 to 256
- own_latent: bfloat16 [4096, 576], P('seq'), may hold values from -16 to 16
- cache: bfloat16 [512, 128, 576], P('seq', 'head'), may hold values from -6 to 6
- block_list: int32 [16, 32], replicated, may hold values from 0 to 511, as said below
- offsets: int32 [16, 32], P('seq'), may hold values from -4096 to 4096
- tile_mask: int32 [16, 2, 32], P('seq'), may hold values 0 or 1
- w_uk: bfloat16 [64, 128, 512], P('head'), may hold values from -0.5 to 0.5
- w_uv: bfloat16 [64, 512, 128], P('head'), may hold values from -0.25 to 0.25
- w_o: bfloat16 [8192, 7168], P('head'), may hold values from -0.0625 to 0.0625
Outputs:
- layer_out: bfloat16 [4096, 7168], P('seq', 'head')
Inputs may be any that keep to these rules, and one draw needn't show every extreme that they name: `block_list`: entry (r, j) names a pooled span whose owner is index entry // 32 of seq. In each row no owner is named more than 4 times, and at least one owner is named exactly 4 times.
All inputs are finite; a program needn't handle non-finite values. No bound on the sum of `tile_mask` on one device may be relied on, other than what follows from the above.
Results may differ from a plain program's by a relative error of at most 0.015.
Values may be sent and summed in bfloat16 or wider, within the bound.
No kernel may reach another device: no remote copies, remote signals or barrier semaphores. Data moves between devices by JAX's collectives and lax.ppermute only.
A program may use at most 128 MiB of HBM per device.

v0:
```python
import functools

import jax
import jax.numpy as jnp
from jax import lax
from jax.experimental import pallas as pl
from jax.experimental.pallas import tpu as pltpu
from jax.sharding import Mesh, PartitionSpec as P


MOST = 4
THETA = 50000.0
TILE = 128
NEG = -1e30
VMEM = pltpu.VMEM
SMEM = pltpu.SMEM


def vspec():
    return pl.BlockSpec(memory_space=VMEM)


def sspec():
    return pl.BlockSpec(memory_space=SMEM)


def params(mib):
    return pltpu.CompilerParams(vmem_limit_bytes=mib * 1024 * 1024)


def cost(flops, moved):
    return pl.CostEstimate(flops=int(flops), bytes_accessed=int(moved), transcendentals=0)


def dot_t(a, b):
    return lax.dot_general(a, b, (((1,), (1,)), ((), ())), preferred_element_type=jnp.float32)


def dot(a, b):
    return jnp.dot(a, b, preferred_element_type=jnp.float32)


def pick_kernel(slot_ref, list_ref, arrived_ref, cos_ref, sin_ref, out_ref):
    latent = out_ref.shape[2] - 64
    for j in range(out_ref.shape[0]):
        rows = arrived_ref[slot_ref[j]]
        out_ref[j, :, :latent] = rows[:, :latent]
        rotary = rows[:, latent:].astype(jnp.float32)
        swapped = jnp.concatenate([rotary[:, 32:], rotary[:, :32]], axis=1)
        turned = rotary * cos_ref[j][None, :] + swapped * sin_ref[j][None, :]
        out_ref[j, :, latent:] = turned.astype(jnp.bfloat16)


def pick(slots, lists, arrived, cosines, sines):
    count = slots.shape[0]
    return pl.pallas_call(
        pick_kernel,
        name="pick",
        out_shape=jax.ShapeDtypeStruct((count,) + arrived.shape[1:], jnp.bfloat16),
        in_specs=[sspec(), sspec(), vspec(), vspec(), vspec()],
        out_specs=vspec(),
        compiler_params=params(4),
        cost_estimate=cost(1e8, 2e6),
    )(slots, lists, arrived, cosines, sines)


def start_kernel(place_ref, mask_ref, q_ref, uk_ref, q_out, list_out):
    heads, nope, latent = uk_ref.shape
    rope = q_out.shape[2] - latent
    width = nope + rope
    tiles = q_ref.shape[0] // TILE
    listed = mask_ref.shape[1]
    room = list_out.shape[1] - 3
    for t in range(tiles):
        for j in range(room):
            list_out[t, j] = 0
        count = jnp.int32(0)
        for j in range(listed):
            list_out[t, count] = j
            count = count + (mask_ref[t, j] > 0).astype(jnp.int32)
        list_out[t, room] = count
        list_out[t, room + 1] = place_ref[0]
        list_out[t, room + 2] = place_ref[1]
    for h in range(heads):
        ql = dot(q_ref[:, h * width : h * width + nope], uk_ref[h]).astype(jnp.bfloat16)
        qr = q_ref[:, h * width + nope : (h + 1) * width]
        for t in range(tiles):
            q_out[t, h * TILE : (h + 1) * TILE, :latent] = ql[t * TILE : (t + 1) * TILE]
            q_out[t, h * TILE : (h + 1) * TILE, latent:] = qr[t * TILE : (t + 1) * TILE]


def start(place, tile_mask, queries, w_uk):
    tiles, listed = tile_mask.shape
    heads, nope, latent = w_uk.shape
    rope = queries.shape[1] // heads - nope
    return pl.pallas_call(
        start_kernel,
        name="start",
        out_shape=(
            jax.ShapeDtypeStruct((tiles, heads * TILE, latent + rope), jnp.bfloat16),
            jax.ShapeDtypeStruct((tiles, listed + 3), jnp.int32),
        ),
        in_specs=[sspec(), sspec(), vspec(), vspec()],
        out_specs=(vspec(), sspec()),
        compiler_params=params(16),
        cost_estimate=cost(4e9, 8e6),
    )(place, tile_mask, queries, w_uk)


def fold(s, v, t, scale, high_ref, sum_ref, acc_ref):
    old = high_ref[t]
    new = jnp.maximum(old, jnp.max(s, axis=1, keepdims=True))
    alpha = jnp.exp((old - new) * scale)
    width = s.shape[1] // 128
    p = jnp.exp((s - jnp.concatenate([new] * width, axis=1)) * scale)
    part = p[:, :128]
    for w in range(1, width):
        part = part + p[:, w * 128 : (w + 1) * 128]
    sum_ref[t] = sum_ref[t] * alpha + part
    high_ref[t] = new
    wide = jnp.concatenate([alpha] * (acc_ref.shape[2] // 128), axis=1)
    acc_ref[t] = acc_ref[t] * wide + dot(p.astype(jnp.bfloat16), v)


def attend(list_ref, q_ref, sources, group, scale, high_ref, sum_ref, acc_ref):
    latent = acc_ref.shape[2]
    tiles = q_ref.shape[0]
    per = len(sources) * sources[0].shape[1]
    room = list_ref.shape[1] - 3
    counts = [list_ref[t, room] for t in range(tiles)]
    most = functools.reduce(jnp.maximum, counts)

    def body(g, carry):
        keys, scores = [], []
        for t in range(tiles):
            rows = jnp.concatenate(
                [ref[list_ref[t, g * group + i]] for i in range(group) for ref in sources], axis=0
            )
            s = dot_t(q_ref[t], rows)
            col = lax.broadcasted_iota(jnp.int32, s.shape, 1)
            keys.append(rows)
            scores.append(jnp.where(col < (counts[t] - g * group) * per, s, NEG))
        for t in range(tiles):
            fold(scores[t], keys[t][:, :latent], t, scale, high_ref, sum_ref, acc_ref)
        return carry

    lax.fori_loop(0, (most + group - 1) // group, body, 0)


def first_kernel(
    list_ref, q_ref, own_ref, *refs, pieces, group, scale
):
    sources = refs[:pieces]
    high_ref, sum_ref, acc_ref = refs[pieces:]
    latent = acc_ref.shape[2]
    for t in range(q_ref.shape[0]):
        keys = own_ref[: (t + 1) * TILE]
        s = dot_t(q_ref[t], keys)
        row = lax.broadcasted_iota(jnp.int32, s.shape, 0) % TILE + t * TILE
        col = lax.broadcasted_iota(jnp.int32, s.shape, 1)
        s = jnp.where(col <= row, s, NEG)
        high = jnp.max(s, axis=1, keepdims=True)
        p = jnp.exp((s - high) * scale)
        part = p[:, :128]
        for w in range(1, t + 1):
            part = part + p[:, w * 128 : (w + 1) * 128]
        high_ref[t] = jnp.broadcast_to(high, high_ref.shape[1:])
        sum_ref[t] = part
        acc_ref[t] = dot(p.astype(jnp.bfloat16), keys[:, :latent])
    attend(list_ref, q_ref, sources, group, scale, high_ref, sum_ref, acc_ref)


def first(lists, q, own_rows, pieces, latent, group, scale):
    tiles, rows, _ = q.shape
    f32 = jnp.float32
    args = (lists, q, own_rows, *pieces)
    return pl.pallas_call(
        functools.partial(first_kernel, pieces=len(pieces), group=group, scale=scale),
        name="first",
        out_shape=(
            jax.ShapeDtypeStruct((tiles, rows, 128), f32),
            jax.ShapeDtypeStruct((tiles, rows, 128), f32),
            jax.ShapeDtypeStruct((tiles, rows, latent), f32),
        ),
        in_specs=[sspec()] + [vspec()] * (len(args) - 1),
        out_specs=(vspec(),) * 3,
        compiler_params=params(16),
        cost_estimate=cost(5e9, 2e7),
    )(*args)


def stage_kernel(list_ref, q_ref, *refs, pieces, group, scale):
    sources = refs[:pieces]
    high_in, sum_in, acc_in, high_ref, sum_ref, acc_ref = refs[pieces:]
    high_ref[...] = high_in[...]
    sum_ref[...] = sum_in[...]
    acc_ref[...] = acc_in[...]
    attend(list_ref, q_ref, sources, group, scale, high_ref, sum_ref, acc_ref)


def stage(lists, q, pieces, state, group, scale, flops):
    first = 2 + len(pieces)
    args = (lists, q, *pieces, *state)
    return pl.pallas_call(
        functools.partial(stage_kernel, pieces=len(pieces), group=group, scale=scale),
        name="stage",
        out_shape=tuple(jax.ShapeDtypeStruct(x.shape, x.dtype) for x in state),
        in_specs=[sspec()] + [vspec()] * (len(args) - 1),
        out_specs=(vspec(),) * 3,
        input_output_aliases={first: 0, first + 1: 1, first + 2: 2},
        compiler_params=params(16),
        cost_estimate=cost(flops, 2e7),
    )(*args)


def project(x, wo_ref, away, mine, list_ref, columns):
    room = list_ref.shape[1] - 3
    level, core = list_ref[0, room + 1], list_ref[0, room + 2]
    core = core if mine else 1 - core
    at = lax.rem(level + away, 4) * (2 * columns) + core * columns
    at = pl.multiple_of(at, 128)
    return dot(x, wo_ref[:, pl.ds(at, columns)]).astype(jnp.bfloat16)


def last_kernel(list_ref, q_ref, *refs, pieces, group, scale):
    halves = refs[:pieces]
    uv_ref, wo_ref, high_in, sum_in, acc_in = refs[pieces : pieces + 5]
    out_ref, mine_ref, other_ref, high_ref, sum_ref, acc_ref, near = refs[pieces + 5 :]
    high_ref[...] = high_in[...]
    sum_ref[...] = sum_in[...]
    acc_ref[...] = acc_in[...]
    spans = halves[0].shape[0]
    for i in range(pieces):
        near[i // 2, (i % 2) * spans : (i % 2 + 1) * spans] = halves[i][...]
    sources = [near.at[i] for i in range(pieces // 2)]
    attend(list_ref, q_ref, sources, group, scale, high_ref, sum_ref, acc_ref)
    for t in range(q_ref.shape[0]):
        total = jnp.sum(sum_ref[t], axis=1, keepdims=True)
        mixed = (acc_ref[t] / total).astype(jnp.bfloat16)
        for h in range(uv_ref.shape[0]):
            out_ref[t * TILE : (t + 1) * TILE, h * 128 : (h + 1) * 128] = dot(
                mixed[h * TILE : (h + 1) * TILE], uv_ref[h]
            ).astype(jnp.bfloat16)
    columns = mine_ref.shape[1]
    x = out_ref[...]
    other_ref[...] = project(x, wo_ref, 2, False, list_ref, columns)
    mine_ref[...] = project(x, wo_ref, 2, True, list_ref, columns)


def last(lists, q, halves, w_uv, state, w_o, group, scale):
    tiles, _, _ = state[2].shape
    tokens = tiles * TILE
    columns = w_o.shape[1] // 8
    bf = jnp.bfloat16
    args = (lists, q, *halves, w_uv, w_o, *state)
    first = len(args) - 3
    shape = halves[0].shape
    outs = pl.pallas_call(
        functools.partial(last_kernel, pieces=len(halves), group=group, scale=scale),
        name="last",
        out_shape=(
            jax.ShapeDtypeStruct((tokens, w_o.shape[0]), bf),
            jax.ShapeDtypeStruct((tokens, columns), bf),
            jax.ShapeDtypeStruct((tokens, columns), bf),
        )
        + tuple(jax.ShapeDtypeStruct(x.shape, x.dtype) for x in state),
        in_specs=[sspec()] + [vspec()] * (len(args) - 1),
        out_specs=(vspec(),) * 6,
        input_output_aliases={first: 3, first + 1: 4, first + 2: 5},
        scratch_shapes=[pltpu.VMEM((len(halves) // 2, 2 * shape[0]) + shape[1:], bf)],
        compiler_params=params(16),
        cost_estimate=cost(8e9, 2e7),
    )(*args)
    return outs[:3]


def rest_kernel(list_ref, x_ref, wo_ref, other_ref, mine_ref):
    columns = other_ref.shape[2]
    x = x_ref[...]
    for i, away in enumerate((1, 3, 0)):
        other_ref[i] = project(x, wo_ref, away, False, list_ref, columns)
    for i, away in enumerate((1, 3, 0)):
        mine_ref[i] = project(x, wo_ref, away, True, list_ref, columns)


def rest(lists, head_out, w_o):
    shape = jax.ShapeDtypeStruct((3, head_out.shape[0], w_o.shape[1] // 8), jnp.bfloat16)
    return pl.pallas_call(
        rest_kernel,
        name="rest",
        out_shape=(shape, shape),
        in_specs=[sspec(), vspec(), vspec()],
        out_specs=(vspec(), vspec()),
        compiler_params=params(8),
        cost_estimate=cost(3e9, 1.2e7),
    )(lists, head_out, w_o)


def per_device(queries, own_latent, cache, block_list, offsets, tile_mask, w_uk, w_uv, w_o):
    seq = ("x", "y")
    seq_count = lax.axis_size(seq)
    seq_index = lax.axis_index(seq)
    spans_held = cache.shape[0]
    latent_full = cache.shape[2]
    listed_count = block_list.shape[1]
    latent = w_uk.shape[2]
    rope = latent_full - latent
    width = w_uk.shape[1] + rope
    scale = width ** (-0.5)

    owners = block_list // spans_held
    within = block_list % spans_held
    earlier = jnp.tril(jnp.ones((listed_count, listed_count), jnp.bool_), -1)
    same_owner = owners[:, :, None] == owners[:, None, :]
    ranking = jnp.sum(same_owner & earlier[None], axis=2)
    slot_ids = jnp.arange(MOST, dtype=jnp.int32)
    matches = (owners == seq_index)[:, :, None] & (ranking[:, :, None] == slot_ids[None, None, :])
    send_index = jnp.sum(jnp.where(matches, within[:, :, None], 0), axis=1)
    my_owners = lax.dynamic_index_in_dim(owners, seq_index, 0, keepdims=False)
    my_ranking = lax.dynamic_index_in_dim(ranking, seq_index, 0, keepdims=False)
    flat_slot = my_owners * MOST + my_ranking
    sent = cache[send_index]
    arrived = lax.all_to_all(sent, seq, split_axis=0, concat_axis=0, tiled=True)

    place = jnp.stack([lax.axis_index("z"), lax.axis_index("c")]).astype(jnp.int32)
    inverse = THETA ** (-jnp.arange(rope // 2, dtype=jnp.float32) * 2.0 / rope)
    angles = offsets[0].astype(jnp.float32)[:, None] * inverse[None, :]
    cosine = jnp.cos(angles)
    sine = jnp.sin(angles)
    cosines = jnp.concatenate([cosine, cosine], axis=1)
    sines = jnp.concatenate([-sine, sine], axis=1)
    q, lists = start(place, tile_mask[0], queries, w_uk)

    own = pick(
        flat_slot,
        lists,
        arrived.reshape(seq_count * MOST, cache.shape[1], latent_full),
        cosines,
        sines,
    )
    size = 4
    up = [(i, (i + 1) % size) for i in range(size)]
    down = [(i, (i - 1) % size) for i in range(size)]
    swap = [(0, 1), (1, 0)]

    def other_core(x):
        return lax.ppermute(x, "c", swap)

    half = own.shape[0] // 2
    plus = lax.ppermute(own, "z", up)
    minus = lax.ppermute(own, "z", down)
    twin = other_core(own)
    state = first(lists, q, own_latent, [own, twin], latent, 16, scale)
    far_low = lax.ppermute(plus[:half], "z", up)
    far_high = lax.ppermute(minus[half:], "z", down)
    pieces = [plus, minus]
    pieces = pieces + [other_core(x) for x in pieces]
    state = stage(lists, q, pieces, state, 8, scale, 1e10)
    halves = [far_low, far_high]
    halves = halves + [other_core(x) for x in halves]
    head_out, far_mine, far_other = last(
        lists, q, halves, w_uv, state, w_o, 16, scale
    )

    bf = jnp.bfloat16
    f32 = jnp.float32

    def add(*terms):
        return functools.reduce(jnp.add, [x.astype(f32) for x in terms])

    h = far_mine.shape[0] // 2
    far = add(far_mine, other_core(far_other)).astype(bf)
    from_below = lax.ppermute(far[:h], "z", up)
    from_above = lax.ppermute(far[h:], "z", down)
    others, mine = rest(lists, head_out, w_o)
    others = other_core(others)
    early_up = lax.ppermute(add(mine[0, h:], others[0, h:]).astype(bf), "z", up)
    early_down = lax.ppermute(add(mine[1, :h], others[1, :h]).astype(bf), "z", down)
    late_up = lax.ppermute(add(mine[0, :h], others[0, :h], from_below).astype(bf), "z", up)
    late_down = lax.ppermute(add(mine[1, h:], others[1, h:], from_above).astype(bf), "z", down)
    kept = add(mine[2], others[2])
    top = add(kept[:h], late_up, early_down)
    bottom = add(kept[h:], early_up, late_down)
    return jnp.concatenate([top, bottom], axis=0).astype(bf)


def solution(mesh):
    fine = Mesh(mesh.devices.reshape(4, 4, 4, 2), ("x", "y", "z", "c"))
    seq = ("x", "y")
    head = ("z", "c")
    placed = (
        P(seq, head),
        P(seq, None),
        P(seq, head, None),
        P(),
        P(seq, None),
        P(seq, None, None),
        P(head, None, None),
        P(head, None, None),
        P(head, None),
    )
    return jax.shard_map(
        per_device, mesh=fine, in_specs=placed, out_specs=P(seq, head), check_vma=False
    )
```

profile of v0, /device:TPU:0, one launch (start us, length us, event | category | flops | bytes accessed | tf_op | source)
XLA Modules:
  0.0 118.8 jit_solution(6224906502091942939)
XLA Ops:
  2.4 1.8 %gather_fusion = bf16[64,16,576]{2,1,0:T(8,128)(2,1)} fusion(bf16[32,16,576]{2,1,0:T(8,128)(2,1)S(1)} %copy-done, s32[1024]{0:T(1024)S(1)} %pad_clamp_fusion), kind=kCustom, calls=%fused_computation | custom fusion | bytes 2359552 | tf_op jit(solution)/shard_map/gather | solution.py:322
  4.2 7.3 %all-to-all-start = ((bf16[16,4,16,576]{3,2,1,0:T(8,128)(2,1)}), bf16[16,4,16,576]{3,2,1,0:T(8,128)(2,1)S(1)}, u32[]{:S(2)}, u32[]{:S(2)}) async-start(bf16[16,4,16,576]{3,2,1,0:T(8,128)(2,1)} %bitcast.5), calls=%async_computation | async-start | bytes 2621440 | tf_op jit(solution)/shard_map/all_to_all | solution.py:323
  11.8 1.2 %copy-done.1 = bf16[8,128,512]{2,1,0:T(8,128)(2,1)S(1)} copy-done((bf16[8,128,512]{2,1,0:T(8,128)(2,1)S(1)}, bf16[8,128,512]{2,1,0:T(8,128)(2,1)}, u32[]{:S(2)}) %copy-start.1) | copy-done | bytes 1048600
  13.0 1.1 copy-done.3
  14.2 2.0 %start.1 = (bf16[2,1024,576]{2,1,0:T(8,128)(2,1)S(1)}, s32[2,35]{1,0:T(2,128)S(1)}) custom-call(s32[2]{0:T(128)S(1)} %pad_add_fusion.place_ref, s32[2,32]{1,0:T(2,128)S(1)} %bitcast.44, bf16[256,1536]{1,0:T(8,128)(2,1)S(1)} %copy-done.3, bf16[8,128,512]{2,1,0:T(8,128)(2,1)S(1)} %copy-done.1), custom_call_target="tpu_custom_call" | custom-call | flops 4000000000 | bytes 8000000 | tf_op jit(solution)/shard_map/start/pallas_call | solution.py:96
  16.2 1.5 %copy-done.5 = bf16[2,1024,576]{2,1,0:T(8,128)(2,1)} copy-done((bf16[2,1024,576]{2,1,0:T(8,128)(2,1)}, bf16[2,1024,576]{2,1,0:T(8,128)(2,1)S(1)}, u32[]{:S(2)}) %copy-start.5) | copy-done | bytes 2359320
  17.6 14.6 %all-to-all-done = bf16[16,4,16,576]{3,2,1,0:T(8,128)(2,1)S(1)} async-done(((bf16[16,4,16,576]{3,2,1,0:T(8,128)(2,1)}), bf16[16,4,16,576]{3,2,1,0:T(8,128)(2,1)S(1)}, u32[]{:S(2)}, u32[]{:S(2)}) %all-to-all-start) | async-done | bytes 1179680 | tf_op jit(solution)/shard_map/all_to_all | solution.py:323
  33.0 2.0 %collective-permute-start = (bf16[32,16,576]{2,1,0:T(8,128)(2,1)S(1)}, bf16[32,16,576]{2,1,0:T(8,128)(2,1)S(1)}, u32[]{:S(2)}, u32[]{:S(2)}) collective-permute-start(bf16[32,16,576]{2,1,0:T(8,128)(2,1)S(1)} %pick.1.refs_0_), channel_id=1, source_target_pairs={{0,2},{2,4},{4,6},{6,0},{1,3},{3,5},{5,7},{7,1},{8,10},{10,12},{12... | collective-permute-start | bytes 1769480 | tf_op jit(solution)/shard_map/ppermute | solution.py:350
  34.9 2.2 %collective-permute-start.2 = (bf16[32,16,576]{2,1,0:T(8,128)(2,1)S(1)}, bf16[32,16,576]{2,1,0:T(8,128)(2,1)S(1)}, u32[]{:S(2)}, u32[]{:S(2)}) collective-permute-start(bf16[32,16,576]{2,1,0:T(8,128)(2,1)S(1)} %pick.1.refs_0_), channel_id=1, source_target_pairs={{0,6},{2,0},{4,2},{6,4},{1,7},{3,1},{5,3},{7,5},{8,14},{10,8},{12,... | collective-permute-start | bytes 1769480 | tf_op jit(solution)/shard_map/ppermute | solution.py:351
  37.1 11.8 %collective-permute-done.refs_0_ = bf16[32,16,576]{2,1,0:T(8,128)(2,1)S(1)} collective-permute-done((bf16[32,16,576]{2,1,0:T(8,128)(2,1)S(1)}, bf16[32,16,576]{2,1,0:T(8,128)(2,1)S(1)}, u32[]{:S(2)}, u32[]{:S(2)}) %collective-permute-start) | collective-permute-done | bytes 589856 | tf_op jit(solution)/shard_map/ppermute | solution.py:350
  49.7 0.8 collective-permute-start.1
  50.6 2.6 %collective-permute-start.3 = (bf16[16,16,576]{2,1,0:T(8,128)(2,1)S(1)}, bf16[16,16,576]{2,1,0:T(8,128)(2,1)S(1)}, u32[]{:S(2)}, u32[]{:S(2)}) collective-permute-start(bf16[16,16,576]{2,1,0:T(8,128)(2,1)S(1)} %slice.75), channel_id=1, source_target_pairs={{0,6},{2,0},{4,2},{6,4},{1,7},{3,1},{5,3},{7,5},{8,14},{10,8},{12,... | collective-permute-start | bytes 884744 | tf_op jit(solution)/shard_map/ppermute | solution.py:355
  53.2 1.7 %copy-done.6 = bf16[2,1024,576]{2,1,0:T(8,128)(2,1)S(1)} copy-done((bf16[2,1024,576]{2,1,0:T(8,128)(2,1)S(1)}, bf16[2,1024,576]{2,1,0:T(8,128)(2,1)}, u32[]{:S(2)}) %copy-start.6) | copy-done | bytes 2359320
  54.9 9.8 %first.1 = (f32[2,1024,128]{2,1,0:T(8,128)S(1)}, f32[2,1024,128]{2,1,0:T(8,128)S(1)}, f32[2,1024,512]{2,1,0:T(8,128)S(1)}) custom-call(s32[2,35]{1,0:T(2,128)S(1)} %get-tuple-element.18.list_ref, bf16[2,1024,576]{2,1,0:T(8,128)(2,1)S(1)} %copy-done.6, bf16[256,576]{1,0:T(8,128)(2,1)S(1)} %copy.21.own_ref, bf16[32,16,576]{2,1,0:T(8,128)(2,1)S(1)} %pick.1.refs_0_, ...), custom_call_target="tpu_custom_call" | custom-call | flops 5000000000 | bytes 20000000 | tf_op jit(solution)/shard_map/first/pallas_call | solution.py:177
  65.4 12.3 %stage.1 = (f32[2,1024,128]{2,1,0:T(8,128)S(1)}, f32[2,1024,128]{2,1,0:T(8,128)S(1)}, f32[2,1024,512]{2,1,0:T(8,128)S(1)}) custom-call(s32[2,35]{1,0:T(2,128)S(1)} %get-tuple-element.18.list_ref, bf16[2,1024,576]{2,1,0:T(8,128)(2,1)S(1)} %copy-done.6, ...), custom_call_target="tpu_custom_call", output_to_operand_aliasing={{0}: (6, {}), {1}: (7, {}), {2}: (8, {})} | custom-call | flops 10000000000 | bytes 20000000 | tf_op jit(solution)/shard_map/stage/pallas_call | solution.py:204
  77.8 9.9 %last.1 = (bf16[256,1024]{1,0:T(8,128)(2,1)S(1)}, bf16[256,896]{1,0:T(8,128)(2,1)S(1)}, bf16[256,896]{1,0:T(8,128)(2,1)S(1)}, f32[2,1024,128]{2,1,0:T(8,128)S(1)...) custom-call(s32[2,35]{1,0:T(2,128)S(1)} %get-tuple-element.18.list_r, ...), custom_call_target="tpu_custom_call", output_to_operand_aliasing={{3}: (8, {}), {4}: (9, {}), {5}: (10, {})} | custom-call | flops 8000000000 | bytes 20000000 | tf_op jit(solution)/shard_map/last/pallas_call | solution.py:258
  87.7 4.0 %rest.1 = (bf16[3,256,896]{2,1,0:T(8,128)(2,1)S(1)}, bf16[3,256,896]{2,1,0:T(8,128)(2,1)S(1)}) custom-call(s32[2,35]{1,0:T(2,128)S(1)} %get-tuple-element.18.list_ref, bf16[256,1024]{1,0:T(8,128)(2,1)S(1)} %get-tuple-element.26.x_ref, bf16[1024,7168]{1,0:T(8,128)(2,1)S(1)} %bitcast.42), custom_call_target="tpu_custom_call" | custom-call | flops 3000000000 | bytes 12000000 | tf_op jit(solution)/shard_map/rest/pallas_call | solution.py:288
  92.3 3.3 %collective-permute-done.10 = bf16[256,896]{1,0:T(8,128)(2,1)S(1)} collective-permute-done((bf16[256,896]{1,0:T(8,128)(2,1)S(1)}, bf16[256,896]{1,0:T(8,128)(2,1)S(1)}, u32[]{:S(2)}, u32[]{:S(2)}) %collective-permute-start.10) | collective-permute-done | bytes 458784 | tf_op jit(solution)/shard_map/ppermute | solution.py:347
  95.8 3.2 %collective-permute-start.15 = (bf16[128,896]{1,0:T(8,128)(2,1)S(1)}, bf16[128,896]{1,0:T(8,128)(2,1)S(1)}, u32[]{:S(2)}, u32[]{:S(2)}) collective-permute-start(bf16[128,896]{1,0:T(8,128)(2,1)S(1)} %get-tuple-element.40), channel_id=1, source_target_pairs={{0,6},{2,0},{4,2},{6,4},{1,7},{3,1},{5,3},{7,5},{8,14},{10,8},{12,... | collective-permute-start | bytes 688136 | tf_op jit(solution)/shard_map/ppermute | solution.py:374
  99.1 5.6 %collective-permute-done.11 = bf16[128,896]{1,0:T(8,128)(2,1)S(1)} collective-permute-done((bf16[128,896]{1,0:T(8,128)(2,1)S(1)}, bf16[128,896]{1,0:T(8,128)(2,1)S(1)}, u32[]{:S(2)}, u32[]{:S(2)}) %collective-permute-start.11) | collective-permute-done | bytes 229408 | tf_op jit(solution)/shard_map/ppermute | solution.py:373
  104.9 3.2 %collective-permute-start.16 = (bf16[128,896]{1,0:T(8,128)(2,1)S(1)}, bf16[128,896]{1,0:T(8,128)(2,1)S(1)}, u32[]{:S(2)}, u32[]{:S(2)}) collective-permute-start(bf16[128,896]{1,0:T(8,128)(2,1)S(1)} %get-tuple-element.34), channel_id=1, source_target_pairs={{0,6},{2,0},{4,2},{6,4},{1,7},{3,1},{5,3},{7,5},{8,14},{10,8},{12,... | collective-permute-start | bytes 688136 | tf_op jit(solution)/shard_map/ppermute | solution.py:380
  108.3 1.8 %collective-permute-start.13 = (bf16[128,896]{1,0:T(8,128)(2,1)S(1)}, bf16[128,896]{1,0:T(8,128)(2,1)S(1)}, u32[]{:S(2)}, u32[]{:S(2)}) collective-permute-start(bf16[128,896]{1,0:T(8,128)(2,1)S(1)} %get-tuple-element.35), channel_id=1, source_target_pairs={{0,6},{2,0},{4,2},{6,4},{1,7},{3,1},{5,3},{7,5},{8,14},{10,8},{12,... | collective-permute-start | bytes 688136 | tf_op jit(solution)/shard_map/ppermute | solution.py:378
  110.5 3.3 %collective-permute-done.12 = bf16[128,896]{1,0:T(8,128)(2,1)S(1)} collective-permute-done((bf16[128,896]{1,0:T(8,128)(2,1)S(1)}, bf16[128,896]{1,0:T(8,128)(2,1)S(1)}, u32[]{:S(2)}, u32[]{:S(2)}) %collective-permute-start.12) | collective-permute-done | bytes 229408 | tf_op jit(solution)/shard_map/ppermute | solution.py:379
  114.2 3.0 %collective-permute-done.13 = bf16[128,896]{1,0:T(8,128)(2,1)S(1)} collective-permute-done((bf16[128,896]{1,0:T(8,128)(2,1)S(1)}, bf16[128,896]{1,0:T(8,128)(2,1)S(1)}, u32[]{:S(2)}, u32[]{:S(2)}) %collective-permute-start.13) | collective-permute-done | bytes 229408 | tf_op jit(solution)/shard_map/ppermute | solution.py:378
  (74 shorter events, 8.4 us)
Async XLA Ops:
  4.2 28.1 %all-to-all-start = ((bf16[16,4,16,576]{3,2,1,0:T(8,128)(2,1)}), bf16[16,4,16,576]{3,2,1,0:T(8,128)(2,1)S(1)}, u32[]{:S(2)}, u32[]{:S(2)}) async-start(bf16[16,4,16,576]{3,2,1,0:T(8,128)(2,1)} %bitcast.5), calls=%async_computation | async-start | bytes 2621440 | tf_op jit(solution)/shard_map/all_to_all | solution.py:323
  17.6 31.9 %copy-start.8 = (bf16[256,576]{0,1:T(8,128)(2,1)S(1)}, bf16[256,576]{0,1:T(8,128)(2,1)}, u32[]{:S(2)}) copy-start(bf16[256,576]{0,1:T(8,128)(2,1)} %param.10) | copy-start | bytes 884740
  33.0 16.0 %collective-permute-start = (bf16[32,16,576]{2,1,0:T(8,128)(2,1)S(1)}, bf16[32,16,576]{2,1,0:T(8,128)(2,1)S(1)}, u32[]{:S(2)}, u32[]{:S(2)}) collective-permute-start(bf16[32,16,576]{2,1,0:T(8,128)(2,1)S(1)} %pick.1.refs_0_), channel_id=1, source_target_pairs={{0,2},{2,4},{4,6},{6,0},{1,3},{3,5},{5,7},{7,1},{8,10},{10,12},{12... | collective-permute-start | bytes 1769480 | tf_op jit(solution)/shard_map/ppermute | solution.py:350
  34.9 14.0 %collective-permute-start.2 = (bf16[32,16,576]{2,1,0:T(8,128)(2,1)S(1)}, bf16[32,16,576]{2,1,0:T(8,128)(2,1)S(1)}, u32[]{:S(2)}, u32[]{:S(2)}) collective-permute-start(bf16[32,16,576]{2,1,0:T(8,128)(2,1)S(1)} %pick.1.refs_0_), channel_id=1, source_target_pairs={{0,6},{2,0},{4,2},{6,4},{1,7},{3,1},{5,3},{7,5},{8,14},{10,8},{12,... | collective-permute-start | bytes 1769480 | tf_op jit(solution)/shard_map/ppermute | solution.py:351
  37.1 16.0 %collective-permute-start.8 = (bf16[32,16,576]{2,1,0:T(8,128)(2,1)S(1)}, bf16[32,16,576]{2,1,0:T(8,128)(2,1)}, u32[]{:S(2)}, u32[]{:S(2)}) collective-permute-start(bf16[32,16,576]{2,1,0:T(8,128)(2,1)S(1)} %pick.1.refs_0_), channel_id=1, source_target_pairs={{0,1},{1,0},{2,3},{3,2},{4,5},{5,4},{6,7},{7,6},{8,9},{9,8},{10,11... | collective-permute-start | bytes 1769480 | tf_op jit(solution)/shard_map/ppermute | solution.py:347
  49.0 16.3 %collective-permute-start.6 = (bf16[32,16,576]{2,1,0:T(8,128)(2,1)S(1)}, bf16[32,16,576]{2,1,0:T(8,128)(2,1)}, u32[]{:S(2)}, u32[]{:S(2)}) collective-permute-start(bf16[32,16,576]{2,1,0:T(8,128)(2,1)S(1)} %collective-permute-done.refs_0_), channel_id=1, source_target_pairs={{0,1},{1,0},{2,3},{3,2},{4,5},{5,4},{6,7},{7,6},{8,9},{9,8},{10,11... | collective-permute-start | bytes 1769480 | tf_op jit(solution)/shard_map/ppermute | solution.py:347
  49.0 16.3 %collective-permute-start.7 = (bf16[32,16,576]{2,1,0:T(8,128)(2,1)S(1)}, bf16[32,16,576]{2,1,0:T(8,128)(2,1)}, u32[]{:S(2)}, u32[]{:S(2)}) collective-permute-start(bf16[32,16,576]{2,1,0:T(8,128)(2,1)S(1)} %collective-permute-done.2.refs_1_), channel_id=1, source_target_pairs={{0,1},{1,0},{2,3},{3,2},{4,5},{5,4},{6,7},{7,6},{8,9},{9,8},{10,11... | collective-permute-start | bytes 1769480 | tf_op jit(solution)/shard_map/ppermute | solution.py:347
  49.7 15.0 %collective-permute-start.1 = (bf16[16,16,576]{2,1,0:T(8,128)(2,1)S(1)}, bf16[16,16,576]{2,1,0:T(8,128)(2,1)S(1)}, u32[]{:S(2)}, u32[]{:S(2)}) collective-permute-start(bf16[16,16,576]{2,1,0:T(8,128)(2,1)S(1)} %slice.74), channel_id=1, source_target_pairs={{0,2},{2,4},{4,6},{6,0},{1,3},{3,5},{5,7},{7,1},{8,10},{10,12},{12... | collective-permute-start | bytes 884744 | tf_op jit(solution)/shard_map/ppermute | solution.py:354
  50.6 14.2 %collective-permute-start.3 = (bf16[16,16,576]{2,1,0:T(8,128)(2,1)S(1)}, bf16[16,16,576]{2,1,0:T(8,128)(2,1)S(1)}, u32[]{:S(2)}, u32[]{:S(2)}) collective-permute-start(bf16[16,16,576]{2,1,0:T(8,128)(2,1)S(1)} %slice.75), channel_id=1, source_target_pairs={{0,6},{2,0},{4,2},{6,4},{1,7},{3,1},{5,3},{7,5},{8,14},{10,8},{12,... | collective-permute-start | bytes 884744 | tf_op jit(solution)/shard_map/ppermute | solution.py:355
  54.9 22.8 %slice-start = ((s8[14680064]{0:T(1024)(128)(4,1)}), s8[4194304]{0:T(1024)(128)(4,1)S(1)}, s32[]{:S(2)}) async-start(s8[14680064]{0:T(1024)(128)(4,1)} %bitcast.41), calls=%async_computation.1 | async-start | bytes 8388608
  54.9 22.8 %slice-start.1 = ((s8[14680064]{0:T(1024)(128)(4,1)}), s8[4194304]{0:T(1024)(128)(4,1)S(1)}, s32[]{:S(2)}) async-start(s8[14680064]{0:T(1024)(128)(4,1)} %bitcast.41), calls=%async_computation.2 | async-start | bytes 8388608
  64.7 13.0 %collective-permute-start.4 = (bf16[16,16,576]{2,1,0:T(8,128)(2,1)S(1)}, bf16[16,16,576]{2,1,0:T(8,128)(2,1)S(1)}, u32[]{:S(2)}, u32[]{:S(2)}) collective-permute-start(bf16[16,16,576]{2,1,0:T(8,128)(2,1)S(1)} %collective-permute-done.1.refs_0_), channel_id=1, source_target_pairs={{0,1},{1,0},{2,3},{3,2},{4,5},{5,4},{6,7},{7,6},{8,9},{9,8},{10,11... | collective-permute-start | bytes 884744 | tf_op jit(solution)/shard_map/ppermute | solution.py:347
  64.8 12.9 %collective-permute-start.5 = (bf16[16,16,576]{2,1,0:T(8,128)(2,1)S(1)}, bf16[16,16,576]{2,1,0:T(8,128)(2,1)S(1)}, u32[]{:S(2)}, u32[]{:S(2)}) collective-permute-start(bf16[16,16,576]{2,1,0:T(8,128)(2,1)S(1)} %collective-permute-done.3.refs_1_), channel_id=1, source_target_pairs={{0,1},{1,0},{2,3},{3,2},{4,5},{5,4},{6,7},{7,6},{8,9},{9,8},{10,11... | collective-permute-start | bytes 884744 | tf_op jit(solution)/shard_map/ppermute | solution.py:347
  65.3 12.4 %slice-start.3 = ((s8[14680064]{0:T(1024)(128)(4,1)}), s8[2097152]{0:T(1024)(128)(4,1)S(1)}, s32[]{:S(2)}) async-start(s8[14680064]{0:T(1024)(128)(4,1)} %bitcast.41), calls=%async_computation.4 | async-start | bytes 4194304
  65.3 12.4 %copy-start.2 = (bf16[8,512,128]{2,1,0:T(8,128)(2,1)S(1)}, bf16[8,512,128]{2,1,0:T(8,128)(2,1)}, u32[]{:S(2)}) copy-start(bf16[8,512,128]{2,1,0:T(8,128)(2,1)} %refs_4_.1) | copy-start | bytes 3145732
  65.4 12.4 %copy-start.7 = (bf16[2,1024,576]{2,1,0:T(8,128)(2,1)S(1)}, bf16[2,1024,576]{2,1,0:T(8,128)(2,1)}, u32[]{:S(2)}) copy-start(bf16[2,1024,576]{2,1,0:T(8,128)(2,1)} %copy-done.5) | copy-start | bytes 7077892
  91.7 13.0 %collective-permute-start.9 = (bf16[3,256,896]{2,1,0:T(8,128)(2,1)S(1)}, bf16[3,256,896]{2,1,0:T(8,128)(2,1)S(1)}, u32[]{:S(2)}, u32[]{:S(2)}) collective-permute-start(bf16[3,256,896]{2,1,0:T(8,128)(2,1)S(1)} %get-tuple-element.28), channel_id=1, source_target_pairs={{0,1},{1,0},{2,3},{3,2},{4,5},{5,4},{6,7},{7,6},{8,9},{9,8},{10,11... | collective-permute-start | bytes 4128776 | tf_op jit(solution)/shard_map/ppermute | solution.py:347
  91.9 3.7 %collective-permute-start.10 = (bf16[256,896]{1,0:T(8,128)(2,1)S(1)}, bf16[256,896]{1,0:T(8,128)(2,1)S(1)}, u32[]{:S(2)}, u32[]{:S(2)}) collective-permute-start(bf16[256,896]{1,0:T(8,128)(2,1)S(1)} %get-tuple-element.30), channel_id=1, source_target_pairs={{0,1},{1,0},{2,3},{3,2},{4,5},{5,4},{6,7},{7,6},{8,9},{9,8},{10,11... | collective-permute-start | bytes 1376264 | tf_op jit(solution)/shard_map/ppermute | solution.py:347
  95.7 8.9 %collective-permute-start.11 = (bf16[128,896]{1,0:T(8,128)(2,1)S(1)}, bf16[128,896]{1,0:T(8,128)(2,1)S(1)}, u32[]{:S(2)}, u32[]{:S(2)}) collective-permute-start(bf16[128,896]{1,0:T(8,128)(2,1)S(1)} %get-tuple-element.39), channel_id=1, source_target_pairs={{0,2},{2,4},{4,6},{6,0},{1,3},{3,5},{5,7},{7,1},{8,10},{10,12},{12... | collective-permute-start | bytes 688136 | tf_op jit(solution)/shard_map/ppermute | solution.py:373
  95.8 8.8 %collective-permute-start.15 = (bf16[128,896]{1,0:T(8,128)(2,1)S(1)}, bf16[128,896]{1,0:T(8,128)(2,1)S(1)}, u32[]{:S(2)}, u32[]{:S(2)}) collective-permute-start(bf16[128,896]{1,0:T(8,128)(2,1)S(1)} %get-tuple-element.40), channel_id=1, source_target_pairs={{0,6},{2,0},{4,2},{6,4},{1,7},{3,1},{5,3},{7,5},{8,14},{10,8},{12,... | collective-permute-start | bytes 688136 | tf_op jit(solution)/shard_map/ppermute | solution.py:374
  104.9 8.9 %collective-permute-start.12 = (bf16[128,896]{1,0:T(8,128)(2,1)S(1)}, bf16[128,896]{1,0:T(8,128)(2,1)S(1)}, u32[]{:S(2)}, u32[]{:S(2)}) collective-permute-start(bf16[128,896]{1,0:T(8,128)(2,1)S(1)} %get-tuple-element.33), channel_id=1, source_target_pairs={{0,2},{2,4},{4,6},{6,0},{1,3},{3,5},{5,7},{7,1},{8,10},{10,12},{12... | collective-permute-start | bytes 688136 | tf_op jit(solution)/shard_map/ppermute | solution.py:379
  104.9 9.2 %collective-permute-start.16 = (bf16[128,896]{1,0:T(8,128)(2,1)S(1)}, bf16[128,896]{1,0:T(8,128)(2,1)S(1)}, u32[]{:S(2)}, u32[]{:S(2)}) collective-permute-start(bf16[128,896]{1,0:T(8,128)(2,1)S(1)} %get-tuple-element.34), channel_id=1, source_target_pairs={{0,6},{2,0},{4,2},{6,4},{1,7},{3,1},{5,3},{7,5},{8,14},{10,8},{12,... | collective-permute-start | bytes 688136 | tf_op jit(solution)/shard_map/ppermute | solution.py:380
  108.3 8.8 %collective-permute-start.13 = (bf16[128,896]{1,0:T(8,128)(2,1)S(1)}, bf16[128,896]{1,0:T(8,128)(2,1)S(1)}, u32[]{:S(2)}, u32[]{:S(2)}) collective-permute-start(bf16[128,896]{1,0:T(8,128)(2,1)S(1)} %get-tuple-element.35), channel_id=1, source_target_pairs={{0,6},{2,0},{4,2},{6,4},{1,7},{3,1},{5,3},{7,5},{8,14},{10,8},{12,... | collective-permute-start | bytes 688136 | tf_op jit(solution)/shard_map/ppermute | solution.py:378
  110.1 7.8 %collective-permute-start.14 = (bf16[128,896]{1,0:T(8,128)(2,1)S(1)}, bf16[128,896]{1,0:T(8,128)(2,1)S(1)}, u32[]{:S(2)}, u32[]{:S(2)}) collective-permute-start(bf16[128,896]{1,0:T(8,128)(2,1)S(1)} %get-tuple-element.36), channel_id=1, source_target_pairs={{0,2},{2,4},{4,6},{6,0},{1,3},{3,5},{5,7},{7,1},{8,10},{10,12},{12... | collective-permute-start | bytes 688136 | tf_op jit(solution)/shard_map/ppermute | solution.py:377
  (8 other events, 35.4 us)
where the time goes:
time: 119 us
  waiting for transfers between devices  42.7 us (36%)
  Pallas kernels  38.8 us (33%)
  starting transfers between devices  25.2 us (21%)
  local copies, waits for them, and re-layouts  7.85 us (7%)
  other arithmetic  3.93 us (3%)
    all_to_all x1, waiting for transfers between devices, per_device(): arrived = lax.all_to_all(sent, seq, split_axis=0, concat_axis=0, tiled=True)  14.6 us
    pallas_call x1, Pallas kernels, stage(): pl.pallas_call(functools.partial(stage_kernel, pieces=len(pieces), group=...  12.3 us
    ppermute x1, waiting for transfers between devices, per_device(): plus = lax.ppermute(own, 'z', up)  11.8 us
    pallas_call x1, Pallas kernels, last(): pl.pallas_call(functools.partial(last_kernel, pieces=len(halves), group=g...  9.88 us
    pallas_call x1, Pallas kernels, first(): pl.pallas_call(functools.partial(first_kernel, pieces=len(pieces), group=...  9.82 us
    all_to_all x1, starting transfers between devices, per_device(): arrived = lax.all_to_all(sent, seq, split_axis=0, concat_axis=0, tiled=True)  7.28 us
    unnamed x29, local copies, waits for them, and re-layouts  5.8 us
    ppermute x1, waiting for transfers between devices, per_device(): from_below = lax.ppermute(far[:h], 'z', up)  5.62 us
  transfers between devices with their start and end apart: 18, of which 8 were waited for; matrix products, arithmetic and copies ran while one was open for 1% of the time, Pallas kernels for 20%

commit v1 on v0

--- a/solution.py
+++ b/solution.py
@@ -107,7 +107,8 @@
     )(place, tile_mask, queries, w_uk)
 
 
-def fold(s, v, t, scale, high_ref, sum_ref, acc_ref):
+def fold(s, v, t, scale, state):
+    high_ref, sum_ref, acc_ref = state
     old = high_ref[t]
     new = jnp.maximum(old, jnp.max(s, axis=1, keepdims=True))
     alpha = jnp.exp((old - new) * scale)
@@ -122,36 +123,64 @@
     acc_ref[t] = acc_ref[t] * wide + dot(p.astype(jnp.bfloat16), v)
 
 
-def attend(list_ref, q_ref, sources, group, scale, high_ref, sum_ref, acc_ref):
-    latent = acc_ref.shape[2]
+def gather(halves, near):
+    spans = halves[0].shape[0]
+    for i, half in enumerate(halves):
+        near[i // 2, (i % 2) * spans : (i % 2 + 1) * spans] = half[...]
+
+
+def attend(list_ref, q_ref, sources, scale, state, short):
+    latent = state[2].shape[2]
     tiles = q_ref.shape[0]
     per = len(sources) * sources[0].shape[1]
+    group = 512 // per
     room = list_ref.shape[1] - 3
     counts = [list_ref[t, room] for t in range(tiles)]
-    most = functools.reduce(jnp.maximum, counts)
-
-    def body(g, carry):
+
+    def step(base, size, which):
         keys, scores = [], []
-        for t in range(tiles):
+        for t in which:
             rows = jnp.concatenate(
-                [ref[list_ref[t, g * group + i]] for i in range(group) for ref in sources], axis=0
+                [ref[list_ref[t, base + i]] for i in range(size) for ref in sources], axis=0
             )
             s = dot_t(q_ref[t], rows)
             col = lax.broadcasted_iota(jnp.int32, s.shape, 1)
             keys.append(rows)
-            scores.append(jnp.where(col < (counts[t] - g * group) * per, s, NEG))
-        for t in range(tiles):
-            fold(scores[t], keys[t][:, :latent], t, scale, high_ref, sum_ref, acc_ref)
+            scores.append(jnp.where(col < (list_ref[t, room] - base) * per, s, NEG))
+        for i, t in enumerate(which):
+            fold(scores[i], keys[i][:, :latent], t, scale, state)
+
+    low, high = jnp.minimum(counts[0], counts[1]), jnp.maximum(counts[0], counts[1])
+    longer = (counts[1] > counts[0]).astype(jnp.int32)
+    full = low // group
+    left = low - full * group
+    wide = left > group // 2 if short else left > 0
+    steps = full + wide.astype(jnp.int32)
+    done = steps * group
+
+    def body(g, carry):
+        step(g * group, group, range(tiles))
         return carry
 
-    lax.fori_loop(0, (most + group - 1) // group, body, 0)
-
-
-def first_kernel(
-    list_ref, q_ref, own_ref, *refs, pieces, group, scale
-):
-    sources = refs[:pieces]
-    high_ref, sum_ref, acc_ref = refs[pieces:]
+    lax.fori_loop(0, steps, body, 0)
+    if short:
+        narrow = jnp.logical_and(left > 0, left <= group // 2)
+        done = done + jnp.where(narrow, group // 2, 0)
+
+        @pl.when(narrow)
+        def _():
+            step(full * group, group // 2, range(tiles))
+
+    def rest_of_longer(g, carry):
+        step(done + g * group, group, (longer,))
+        return carry
+
+    lax.fori_loop(0, (jnp.maximum(high - done, 0) + group - 1) // group, rest_of_longer, 0)
+
+
+def first_kernel(list_ref, q_ref, own_ref, *refs, pieces, scale):
+    sources, state = refs[:pieces], refs[pieces:]
+    high_ref, sum_ref, acc_ref = state
     latent = acc_ref.shape[2]
     for t in range(q_ref.shape[0]):
         keys = own_ref[: (t + 1) * TILE]
@@ -167,15 +196,20 @@
         high_ref[t] = jnp.broadcast_to(high, high_ref.shape[1:])
         sum_ref[t] = part
         acc_ref[t] = dot(p.astype(jnp.bfloat16), keys[:, :latent])
-    attend(list_ref, q_ref, sources, group, scale, high_ref, sum_ref, acc_ref)
-
-
-def first(lists, q, own_rows, pieces, latent, group, scale):
+    attend(list_ref, q_ref, sources, scale, state, False)
+
+
+def near_scratch(halves):
+    shape = halves[0].shape
+    return pltpu.VMEM((len(halves) // 2, 2 * shape[0]) + shape[1:], halves[0].dtype)
+
+
+def first(lists, q, own_rows, halves, latent, scale):
     tiles, rows, _ = q.shape
     f32 = jnp.float32
-    args = (lists, q, own_rows, *pieces)
-    return pl.pallas_call(
-        functools.partial(first_kernel, pieces=len(pieces), group=group, scale=scale),
+    args = (lists, q, own_rows, *halves)
+    return pl.pallas_call(
+        functools.partial(first_kernel, pieces=len(halves), scale=scale),
         name="first",
         out_shape=(
             jax.ShapeDtypeStruct((tiles, rows, 128), f32),
@@ -189,27 +223,26 @@
     )(*args)
 
 
-def stage_kernel(list_ref, q_ref, *refs, pieces, group, scale):
+def stage_kernel(list_ref, q_ref, *refs, pieces, scale):
     sources = refs[:pieces]
-    high_in, sum_in, acc_in, high_ref, sum_ref, acc_ref = refs[pieces:]
-    high_ref[...] = high_in[...]
-    sum_ref[...] = sum_in[...]
-    acc_ref[...] = acc_in[...]
-    attend(list_ref, q_ref, sources, group, scale, high_ref, sum_ref, acc_ref)
-
-
-def stage(lists, q, pieces, state, group, scale, flops):
-    first = 2 + len(pieces)
-    args = (lists, q, *pieces, *state)
-    return pl.pallas_call(
-        functools.partial(stage_kernel, pieces=len(pieces), group=group, scale=scale),
+    source, state = refs[pieces : pieces + 3], refs[pieces + 3 : pieces + 6]
+    for old, new in zip(source, state):
+        new[...] = old[...]
+    attend(list_ref, q_ref, sources, scale, state, True)
+
+
+def stage(lists, q, halves, state, scale):
+    before = 2 + len(halves)
+    args = (lists, q, *halves, *state)
+    return pl.pallas_call(
+        functools.partial(stage_kernel, pieces=len(halves), scale=scale),
         name="stage",
         out_shape=tuple(jax.ShapeDtypeStruct(x.shape, x.dtype) for x in state),
         in_specs=[sspec()] + [vspec()] * (len(args) - 1),
         out_specs=(vspec(),) * 3,
-        input_output_aliases={first: 0, first + 1: 1, first + 2: 2},
-        compiler_params=params(16),
-        cost_estimate=cost(flops, 2e7),
+        input_output_aliases={before: 0, before + 1: 1, before + 2: 2},
+        compiler_params=params(18),
+        cost_estimate=cost(1e10, 2e7),
     )(*args)
 
 
@@ -222,21 +255,20 @@
     return dot(x, wo_ref[:, pl.ds(at, columns)]).astype(jnp.bfloat16)
 
 
-def last_kernel(list_ref, q_ref, *refs, pieces, group, scale):
+def last_kernel(list_ref, q_ref, *refs, pieces, scale):
     halves = refs[:pieces]
-    uv_ref, wo_ref, high_in, sum_in, acc_in = refs[pieces : pieces + 5]
-    out_ref, mine_ref, other_ref, high_ref, sum_ref, acc_ref, near = refs[pieces + 5 :]
-    high_ref[...] = high_in[...]
-    sum_ref[...] = sum_in[...]
-    acc_ref[...] = acc_in[...]
-    spans = halves[0].shape[0]
-    for i in range(pieces):
-        near[i // 2, (i % 2) * spans : (i % 2 + 1) * spans] = halves[i][...]
-    sources = [near.at[i] for i in range(pieces // 2)]
-    attend(list_ref, q_ref, sources, group, scale, high_ref, sum_ref, acc_ref)
+    uv_ref, wo_ref = refs[pieces : pieces + 2]
+    source = refs[pieces + 2 : pieces + 5]
+    out_ref, mine_ref, other_ref = refs[pieces + 5 : pieces + 8]
+    state, near = refs[pieces + 8 : pieces + 11], refs[pieces + 11]
+    gather(halves, near)
+    for old, new in zip(source, state):
+        new[...] = old[...]
+    sources = [near.at[i] for i in range(near.shape[0])]
+    attend(list_ref, q_ref, sources, scale, state, True)
     for t in range(q_ref.shape[0]):
-        total = jnp.sum(sum_ref[t], axis=1, keepdims=True)
-        mixed = (acc_ref[t] / total).astype(jnp.bfloat16)
+        total = jnp.sum(state[1][t], axis=1, keepdims=True)
+        mixed = (state[2][t] / total).astype(jnp.bfloat16)
         for h in range(uv_ref.shape[0]):
             out_ref[t * TILE : (t + 1) * TILE, h * 128 : (h + 1) * 128] = dot(
                 mixed[h * TILE : (h + 1) * TILE], uv_ref[h]
@@ -247,16 +279,15 @@
     mine_ref[...] = project(x, wo_ref, 2, True, list_ref, columns)
 
 
-def last(lists, q, halves, w_uv, state, w_o, group, scale):
+def last(lists, q, halves, w_uv, state, w_o, scale):
     tiles, _, _ = state[2].shape
     tokens = tiles * TILE
     columns = w_o.shape[1] // 8
     bf = jnp.bfloat16
     args = (lists, q, *halves, w_uv, w_o, *state)
-    first = len(args) - 3
-    shape = halves[0].shape
+    before = len(args) - 3
     outs = pl.pallas_call(
-        functools.partial(last_kernel, pieces=len(halves), group=group, scale=scale),
+        functools.partial(last_kernel, pieces=len(halves), scale=scale),
         name="last",
         out_shape=(
             jax.ShapeDtypeStruct((tokens, w_o.shape[0]), bf),
@@ -266,34 +297,59 @@
         + tuple(jax.ShapeDtypeStruct(x.shape, x.dtype) for x in state),
         in_specs=[sspec()] + [vspec()] * (len(args) - 1),
         out_specs=(vspec(),) * 6,
-        input_output_aliases={first: 3, first + 1: 4, first + 2: 5},
-        scratch_shapes=[pltpu.VMEM((len(halves) // 2, 2 * shape[0]) + shape[1:], bf)],
+        input_output_aliases={before: 3, before + 1: 4, before + 2: 5},
+        scratch_shapes=[near_scratch(halves)],
         compiler_params=params(16),
         cost_estimate=cost(8e9, 2e7),
     )(*args)
     return outs[:3]
 
 
-def rest_kernel(list_ref, x_ref, wo_ref, other_ref, mine_ref):
+def columns_kernel(list_ref, x_ref, wo_ref, other_ref, mine_ref, *, aways):
     columns = other_ref.shape[2]
     x = x_ref[...]
-    for i, away in enumerate((1, 3, 0)):
+    for i, away in enumerate(aways):
         other_ref[i] = project(x, wo_ref, away, False, list_ref, columns)
-    for i, away in enumerate((1, 3, 0)):
+    for i, away in enumerate(aways):
         mine_ref[i] = project(x, wo_ref, away, True, list_ref, columns)
 
 
-def rest(lists, head_out, w_o):
-    shape = jax.ShapeDtypeStruct((3, head_out.shape[0], w_o.shape[1] // 8), jnp.bfloat16)
-    return pl.pallas_call(
-        rest_kernel,
-        name="rest",
+def columns_of(lists, head_out, w_o, aways):
+    tokens = head_out.shape[0]
+    shape = jax.ShapeDtypeStruct((len(aways), tokens, w_o.shape[1] // 8), jnp.bfloat16)
+    return pl.pallas_call(
+        functools.partial(columns_kernel, aways=aways),
+        name="columns",
         out_shape=(shape, shape),
         in_specs=[sspec(), vspec(), vspec()],
         out_specs=(vspec(), vspec()),
         compiler_params=params(8),
-        cost_estimate=cost(3e9, 1.2e7),
+        cost_estimate=cost(1e9 * len(aways), 4e6 * len(aways)),
     )(lists, head_out, w_o)
+
+
+def finish_kernel(mine_ref, other_ref, *refs):
+    out_ref = refs[-1]
+    half = refs[0].shape[0]
+    f32 = jnp.float32
+    for i in range(2):
+        rows = pl.ds(i * half, half)
+        total = mine_ref[0, rows].astype(f32) + other_ref[0, rows].astype(f32)
+        for ref in refs[2 * i : 2 * i + 2]:
+            total = total + ref[...].astype(f32)
+        out_ref[rows] = total.astype(jnp.bfloat16)
+
+
+def finish(mine, other, top, bottom):
+    args = (mine, other, *top, *bottom)
+    return pl.pallas_call(
+        finish_kernel,
+        name="finish",
+        out_shape=jax.ShapeDtypeStruct(mine.shape[1:], jnp.bfloat16),
+        in_specs=[vspec()] * len(args),
+        out_specs=vspec(),
+        compiler_params=params(8),
+    )(*args)
 
 
 def per_device(queries, own_latent, cache, block_list, offsets, tile_mask, w_uk, w_uv, w_o):
@@ -301,8 +357,8 @@
     seq_count = lax.axis_size(seq)
     seq_index = lax.axis_index(seq)
     spans_held = cache.shape[0]
+    listed_count = block_list.shape[1]
     latent_full = cache.shape[2]
-    listed_count = block_list.shape[1]
     latent = w_uk.shape[2]
     rope = latent_full - latent
     width = w_uk.shape[1] + rope
@@ -346,21 +402,22 @@
     def other_core(x):
         return lax.ppermute(x, "c", swap)
 
+    def move(x, ways):
+        return lax.ppermute(x, "z", ways)
+
+    plus = move(own, up)
+    minus = move(own, down)
+    twin = other_core(own)
+    state = first(lists, q, own_latent, [own, twin], latent, scale)
     half = own.shape[0] // 2
-    plus = lax.ppermute(own, "z", up)
-    minus = lax.ppermute(own, "z", down)
-    twin = other_core(own)
-    state = first(lists, q, own_latent, [own, twin], latent, 16, scale)
-    far_low = lax.ppermute(plus[:half], "z", up)
-    far_high = lax.ppermute(minus[half:], "z", down)
+    low = move(plus[:half], up)
+    high = move(minus[half:], down)
     pieces = [plus, minus]
     pieces = pieces + [other_core(x) for x in pieces]
-    state = stage(lists, q, pieces, state, 8, scale, 1e10)
-    halves = [far_low, far_high]
+    state = stage(lists, q, pieces, state, scale)
+    halves = [low, high]
     halves = halves + [other_core(x) for x in halves]
-    head_out, far_mine, far_other = last(
-        lists, q, halves, w_uv, state, w_o, 16, scale
-    )
+    head_out, far_mine, far_other = last(lists, q, halves, w_uv, state, w_o, scale)
 
     bf = jnp.bfloat16
     f32 = jnp.float32
@@ -369,19 +426,19 @@
         return functools.reduce(jnp.add, [x.astype(f32) for x in terms])
 
     h = far_mine.shape[0] // 2
-    far = add(far_mine, other_core(far_other)).astype(bf)
-    from_below = lax.ppermute(far[:h], "z", up)
-    from_above = lax.ppermute(far[h:], "z", down)
-    others, mine = rest(lists, head_out, w_o)
+    far_other = other_core(far_other)
+    others, mine = columns_of(lists, head_out, w_o, (1, 3))
     others = other_core(others)
-    early_up = lax.ppermute(add(mine[0, h:], others[0, h:]).astype(bf), "z", up)
-    early_down = lax.ppermute(add(mine[1, :h], others[1, :h]).astype(bf), "z", down)
-    late_up = lax.ppermute(add(mine[0, :h], others[0, :h], from_below).astype(bf), "z", up)
-    late_down = lax.ppermute(add(mine[1, h:], others[1, h:], from_above).astype(bf), "z", down)
-    kept = add(mine[2], others[2])
-    top = add(kept[:h], late_up, early_down)
-    bottom = add(kept[h:], early_up, late_down)
-    return jnp.concatenate([top, bottom], axis=0).astype(bf)
+    far = add(far_mine, far_other).astype(bf)
+    below = move(far[:h], up)
+    above = move(far[h:], down)
+    early_up = move(add(mine[0, h:], others[0, h:]).astype(bf), up)
+    early_down = move(add(mine[1, :h], others[1, :h]).astype(bf), down)
+    kept_other, kept_mine = columns_of(lists, head_out, w_o, (0,))
+    late_up = move(add(mine[0, :h], others[0, :h], below).astype(bf), up)
+    late_down = move(add(mine[1, h:], others[1, h:], above).astype(bf), down)
+    kept_other = other_core(kept_other)
+    return finish(kept_mine, kept_other, (late_up, early_down), (early_up, late_down))
 
 
 def solution(mesh):

time: 119 us -> 112 us (0.941)
  the two profiles are of different devices: /device:TPU:0 before, /device:TPU:8 now
where the time goes in v1:
time: 112 us
  Pallas kernels  39.9 us (36%)
  waiting for transfers between devices  34.7 us (31%)
  starting transfers between devices  25.8 us (23%)
  local copies, waits for them, and re-layouts  7.87 us (7%)
  other arithmetic  2.89 us (3%)
    ppermute x10, waiting for transfers between devices, move(): return lax.ppermute(x, 'z', ways)  21.5 us
    ppermute x10, starting transfers between devices, move(): return lax.ppermute(x, 'z', ways)  16.3 us
    all_to_all x1, waiting for transfers between devices, per_device(): arrived = lax.all_to_all(sent, seq, split_axis=0, concat_axis=0, tiled=True)  13.3 us
    pallas_call x1, Pallas kernels, stage(): pl.pallas_call(functools.partial(stage_kernel, pieces=len(halves), scale=...  12.7 us
    pallas_call x1, Pallas kernels, first(): pl.pallas_call(functools.partial(first_kernel, pieces=len(halves), scale=...  9.8 us
    pallas_call x1, Pallas kernels, last(): pl.pallas_call(functools.partial(last_kernel, pieces=len(halves), scale=s...  8.94 us
    all_to_all x1, starting transfers between devices, per_device(): arrived = lax.all_to_all(sent, seq, split_axis=0, concat_axis=0, tiled=True)  7.39 us
    unnamed x29, local copies, waits for them, and re-layouts  5.81 us
  transfers between devices with their start and end apart: 19, of which 6 were waited for; matrix products, arithmetic and copies ran while one was open for 1% of the time, Pallas kernels for 26%

profile of v1, /device:TPU:8, one launch (start us, length us, event | category | flops | bytes accessed | tf_op | source)
XLA Modules:
  0.0 111.6 jit_solution(11756075457638131521)
XLA Ops:
  2.4 1.8 %gather_fusion = bf16[64,16,576]{2,1,0:T(8,128)(2,1)} fusion(bf16[32,16,576]{2,1,0:T(8,128)(2,1)S(1)} %copy-done, s32[1024]{0:T(1024)S(1)} %pad_clamp_fusion), kind=kCustom, calls=%fused_computation | custom fusion | bytes 2359552 | tf_op jit(solution)/shard_map/gather | solution.py:378
  4.2 7.4 %all-to-all-start = ((bf16[16,4,16,576]{3,2,1,0:T(8,128)(2,1)}), bf16[16,4,16,576]{3,2,1,0:T(8,128)(2,1)S(1)}, u32[]{:S(2)}, u32[]{:S(2)}) async-start(bf16[16,4,16,576]{3,2,1,0:T(8,128)(2,1)} %bitcast.5), calls=%async_computation | async-start | bytes 2621440 | tf_op jit(solution)/shard_map/all_to_all | solution.py:379
  11.9 1.2 %copy-done.1 = bf16[8,128,512]{2,1,0:T(8,128)(2,1)S(1)} copy-done((bf16[8,128,512]{2,1,0:T(8,128)(2,1)S(1)}, bf16[8,128,512]{2,1,0:T(8,128)(2,1)}, u32[]{:S(2)}) %copy-start.1) | copy-done | bytes 1048600
  13.2 1.1 %copy-done.3 = bf16[256,1536]{1,0:T(8,128)(2,1)S(1)} copy-done((bf16[256,1536]{1,0:T(8,128)(2,1)S(1)}, bf16[256,1536]{1,0:T(8,128)(2,1)}, u32[]{:S(2)}) %copy-start.3) | copy-done | bytes 786456
  14.3 2.0 %start.1 = (bf16[2,1024,576]{2,1,0:T(8,128)(2,1)S(1)}, s32[2,35]{1,0:T(2,128)S(1)}) custom-call(s32[2]{0:T(128)S(1)} %pad_add_fusion.place_ref, s32[2,32]{1,0:T(2,128)S(1)} %bitcast.28, bf16[256,1536]{1,0:T(8,128)(2,1)S(1)} %copy-done.3, bf16[8,128,512]{2,1,0:T(8,128)(2,1)S(1)} %copy-done.1), custom_call_target="tpu_custom_call" | custom-call | flops 4000000000 | bytes 8000000 | tf_op jit(solution)/shard_map/start/pallas_call | solution.py:96
  16.3 1.5 %copy-done.5 = bf16[2,1024,576]{2,1,0:T(8,128)(2,1)} copy-done((bf16[2,1024,576]{2,1,0:T(8,128)(2,1)}, bf16[2,1024,576]{2,1,0:T(8,128)(2,1)S(1)}, u32[]{:S(2)}) %copy-start.5) | copy-done | bytes 2359320
  17.8 13.3 %all-to-all-done = bf16[16,4,16,576]{3,2,1,0:T(8,128)(2,1)S(1)} async-done(((bf16[16,4,16,576]{3,2,1,0:T(8,128)(2,1)}), bf16[16,4,16,576]{3,2,1,0:T(8,128)(2,1)S(1)}, u32[]{:S(2)}, u32[]{:S(2)}) %all-to-all-start) | async-done | bytes 1179680 | tf_op jit(solution)/shard_map/all_to_all | solution.py:379
  31.7 2.0 %collective-permute-start = (bf16[32,16,576]{2,1,0:T(8,128)(2,1)S(1)}, bf16[32,16,576]{2,1,0:T(8,128)(2,1)S(1)}, u32[]{:S(2)}, u32[]{:S(2)}) collective-permute-start(bf16[32,16,576]{2,1,0:T(8,128)(2,1)S(1)} %pick.1.refs_0_), channel_id=1, source_target_pairs={{0,2},{2,4},{4,6},{6,0},{1,3},{3,5},{5,7},{7,1},{8,10},{10,12},{12... | collective-permute-start | bytes 1769480 | tf_op jit(solution)/shard_map/ppermute | solution.py:406
  33.7 2.2 %collective-permute-start.2 = (bf16[32,16,576]{2,1,0:T(8,128)(2,1)S(1)}, bf16[32,16,576]{2,1,0:T(8,128)(2,1)S(1)}, u32[]{:S(2)}, u32[]{:S(2)}) collective-permute-start(bf16[32,16,576]{2,1,0:T(8,128)(2,1)S(1)} %pick.1.refs_0_), channel_id=1, source_target_pairs={{0,6},{2,0},{4,2},{6,4},{1,7},{3,1},{5,3},{7,5},{8,14},{10,8},{12,... | collective-permute-start | bytes 1769480 | tf_op jit(solution)/shard_map/ppermute | solution.py:406
  35.9 11.7 %collective-permute-done.refs_0_ = bf16[32,16,576]{2,1,0:T(8,128)(2,1)S(1)} collective-permute-done((bf16[32,16,576]{2,1,0:T(8,128)(2,1)S(1)}, bf16[32,16,576]{2,1,0:T(8,128)(2,1)S(1)}, u32[]{:S(2)}, u32[]{:S(2)}) %collective-permute-start) | collective-permute-done | bytes 589856 | tf_op jit(solution)/shard_map/ppermute | solution.py:406
  49.2 2.6 %collective-permute-start.3 = (bf16[16,16,576]{2,1,0:T(8,128)(2,1)S(1)}, bf16[16,16,576]{2,1,0:T(8,128)(2,1)S(1)}, u32[]{:S(2)}, u32[]{:S(2)}) collective-permute-start(bf16[16,16,576]{2,1,0:T(8,128)(2,1)S(1)} %slice.51), channel_id=1, source_target_pairs={{0,6},{2,0},{4,2},{6,4},{1,7},{3,1},{5,3},{7,5},{8,14},{10,8},{12,... | collective-permute-start | bytes 884744 | tf_op jit(solution)/shard_map/ppermute | solution.py:406
  51.8 1.7 %copy-done.6 = bf16[2,1024,576]{2,1,0:T(8,128)(2,1)S(1)} copy-done((bf16[2,1024,576]{2,1,0:T(8,128)(2,1)S(1)}, bf16[2,1024,576]{2,1,0:T(8,128)(2,1)}, u32[]{:S(2)}) %copy-start.6) | copy-done | bytes 2359320
  53.5 9.8 %first.1 = (f32[2,1024,128]{2,1,0:T(8,128)S(1)}, f32[2,1024,128]{2,1,0:T(8,128)S(1)}, f32[2,1024,512]{2,1,0:T(8,128)S(1)}) custom-call(s32[2,35]{1,0:T(2,128)S(1)} %get-tuple-element.20.list_ref, bf16[2,1024,576]{2,1,0:T(8,128)(2,1)S(1)} %copy-done.6, bf16[256,576]{1,0:T(8,128)(2,1)S(1)} %copy.21.own_ref, bf16[32,16,576]{2,1,0:T(8,128)(2,1)S(1)} %pick.1.refs_0_, ...), custom_call_target="tpu_custom_call" | custom-call | flops 5000000000 | bytes 20000000 | tf_op jit(solution)/shard_map/first/pallas_call | solution.py:211
  64.0 12.7 %stage.1 = (f32[2,1024,128]{2,1,0:T(8,128)S(1)}, f32[2,1024,128]{2,1,0:T(8,128)S(1)}, f32[2,1024,512]{2,1,0:T(8,128)S(1)}) custom-call(s32[2,35]{1,0:T(2,128)S(1)} %get-tuple-element.20.list_ref, bf16[2,1024,576]{2,1,0:T(8,128)(2,1)S(1)} %copy-done.7, ...), custom_call_target="tpu_custom_call", output_to_operand_aliasing={{0}: (6, {}), {1}: (7, {}), {2}: (8, {})} | custom-call | flops 10000000000 | bytes 20000000 | tf_op jit(solution)/shard_map/stage/pallas_call | solution.py:237
  76.8 8.9 %last.1 = (bf16[256,1024]{1,0:T(8,128)(2,1)S(1)}, bf16[256,896]{1,0:T(8,128)(2,1)S(1)}, bf16[256,896]{1,0:T(8,128)(2,1)S(1)}, f32[2,1024,128]{2,1,0:T(8,128)S(1)...) custom-call(s32[2,35]{1,0:T(2,128)S(1)} %get-tuple-element.20.list_r, ...), custom_call_target="tpu_custom_call", output_to_operand_aliasing={{3}: (8, {}), {4}: (9, {}), {5}: (10, {})} | custom-call | flops 8000000000 | bytes 20000000 | tf_op jit(solution)/shard_map/last/pallas_call | solution.py:289
  86.1 2.9 %columns.3 = (bf16[2,256,896]{2,1,0:T(8,128)(2,1)S(1)}, bf16[2,256,896]{2,1,0:T(8,128)(2,1)S(1)}) custom-call(s32[2,35]{1,0:T(2,128)S(1)} %get-tuple-element.20.list_ref, bf16[256,1024]{1,0:T(8,128)(2,1)S(1)} %get-tuple-element.28.x_ref, bf16[1024,7168]{1,0:T(8,128)(2,1)S(1)} %bitcast.26), custom_call_target="tpu_custom_call" | custom-call | flops 2000000000 | bytes 8000000 | tf_op jit(solution)/shard_map/columns/pallas_call | solution.py:320
  89.4 1.8 %columns.2 = (bf16[1,256,896]{2,1,0:T(8,128)(2,1)S(1)}, bf16[1,256,896]{2,1,0:T(8,128)(2,1)S(1)}) custom-call(s32[2,35]{1,0:T(2,128)S(1)} %get-tuple-element.20.list_ref, bf16[256,1024]{1,0:T(8,128)(2,1)S(1)} %get-tuple-element.28.x_ref, bf16[1024,7168]{1,0:T(8,128)(2,1)S(1)} %bitcast.26), custom_call_target="tpu_custom_call" | custom-call | flops 1000000000 | bytes 4000000 | tf_op jit(solution)/shard_map/columns/pallas_call | solution.py:320
  91.8 3.2 %collective-permute-start.16 = (bf16[128,896]{1,0:T(8,128)(2,1)S(1)}, bf16[128,896]{1,0:T(8,128)(2,1)S(1)}, u32[]{:S(2)}, u32[]{:S(2)}) collective-permute-start(bf16[128,896]{1,0:T(8,128)(2,1)S(1)} %get-tuple-element.41), channel_id=1, source_target_pairs={{0,6},{2,0},{4,2},{6,4},{1,7},{3,1},{5,3},{7,5},{8,14},{10,8},{12,... | collective-permute-start | bytes 688136 | tf_op jit(solution)/shard_map/ppermute | solution.py:406
  95.3 2.0 %collective-permute-start.15 = (bf16[128,896]{1,0:T(8,128)(2,1)S(1)}, bf16[128,896]{1,0:T(8,128)(2,1)S(1)}, u32[]{:S(2)}, u32[]{:S(2)}) collective-permute-start(bf16[128,896]{1,0:T(8,128)(2,1)S(1)} %get-tuple-element.39), channel_id=1, source_target_pairs={{0,2},{2,4},{4,6},{6,0},{1,3},{3,5},{5,7},{7,1},{8,10},{10,12},{12... | collective-permute-start | bytes 688136 | tf_op jit(solution)/shard_map/ppermute | solution.py:406
  97.2 4.2 %collective-permute-done.12 = bf16[128,896]{1,0:T(8,128)(2,1)S(1)} collective-permute-done((bf16[128,896]{1,0:T(8,128)(2,1)S(1)}, bf16[128,896]{1,0:T(8,128)(2,1)S(1)}, u32[]{:S(2)}, u32[]{:S(2)}) %collective-permute-start.12) | collective-permute-done | bytes 229408 | tf_op jit(solution)/shard_map/ppermute | solution.py:406
  101.7 3.3 %collective-permute-start.17 = (bf16[128,896]{1,0:T(8,128)(2,1)S(1)}, bf16[128,896]{1,0:T(8,128)(2,1)S(1)}, u32[]{:S(2)}, u32[]{:S(2)}) collective-permute-start(bf16[128,896]{1,0:T(8,128)(2,1)S(1)} %get-tuple-element.37), channel_id=1, source_target_pairs={{0,6},{2,0},{4,2},{6,4},{1,7},{3,1},{5,3},{7,5},{8,14},{10,8},{12,... | collective-permute-start | bytes 688136 | tf_op jit(solution)/shard_map/ppermute | solution.py:406
  105.0 0.9 collective-permute-done.14.refs_1_
  106.4 4.2 %collective-permute-done.13.refs_0_ = bf16[128,896]{1,0:T(8,128)(2,1)S(1)} collective-permute-done((bf16[128,896]{1,0:T(8,128)(2,1)S(1)}, bf16[128,896]{1,0:T(8,128)(2,1)S(1)}, u32[]{:S(2)}, u32[]{:S(2)}) %collective-permute-start.13) | collective-permute-done | bytes 229408 | tf_op jit(solution)/shard_map/ppermute | solution.py:406
  110.6 1.0 finish.1
  (75 shorter events, 7.8 us)
Async XLA Ops:
  4.2 26.8 %all-to-all-start = ((bf16[16,4,16,576]{3,2,1,0:T(8,128)(2,1)}), bf16[16,4,16,576]{3,2,1,0:T(8,128)(2,1)S(1)}, u32[]{:S(2)}, u32[]{:S(2)}) async-start(bf16[16,4,16,576]{3,2,1,0:T(8,128)(2,1)} %bitcast.5), calls=%async_computation | async-start | bytes 2621440 | tf_op jit(solution)/shard_map/all_to_all | solution.py:379
  14.3 33.8 %copy-start.8 = (bf16[256,576]{0,1:T(8,128)(2,1)S(1)}, bf16[256,576]{0,1:T(8,128)(2,1)}, u32[]{:S(2)}) copy-start(bf16[256,576]{0,1:T(8,128)(2,1)} %param.10) | copy-start | bytes 884740
  31.7 15.9 %collective-permute-start = (bf16[32,16,576]{2,1,0:T(8,128)(2,1)S(1)}, bf16[32,16,576]{2,1,0:T(8,128)(2,1)S(1)}, u32[]{:S(2)}, u32[]{:S(2)}) collective-permute-start(bf16[32,16,576]{2,1,0:T(8,128)(2,1)S(1)} %pick.1.refs_0_), channel_id=1, source_target_pairs={{0,2},{2,4},{4,6},{6,0},{1,3},{3,5},{5,7},{7,1},{8,10},{10,12},{12... | collective-permute-start | bytes 1769480 | tf_op jit(solution)/shard_map/ppermute | solution.py:406
  33.7 13.9 %collective-permute-start.2 = (bf16[32,16,576]{2,1,0:T(8,128)(2,1)S(1)}, bf16[32,16,576]{2,1,0:T(8,128)(2,1)S(1)}, u32[]{:S(2)}, u32[]{:S(2)}) collective-permute-start(bf16[32,16,576]{2,1,0:T(8,128)(2,1)S(1)} %pick.1.refs_0_), channel_id=1, source_target_pairs={{0,6},{2,0},{4,2},{6,4},{1,7},{3,1},{5,3},{7,5},{8,14},{10,8},{12,... | collective-permute-start | bytes 1769480 | tf_op jit(solution)/shard_map/ppermute | solution.py:406
  35.9 15.9 %collective-permute-start.8 = (bf16[32,16,576]{2,1,0:T(8,128)(2,1)S(1)}, bf16[32,16,576]{2,1,0:T(8,128)(2,1)}, u32[]{:S(2)}, u32[]{:S(2)}) collective-permute-start(bf16[32,16,576]{2,1,0:T(8,128)(2,1)S(1)} %pick.1.refs_0_), channel_id=1, source_target_pairs={{0,1},{1,0},{2,3},{3,2},{4,5},{5,4},{6,7},{7,6},{8,9},{9,8},{10,11... | collective-permute-start | bytes 1769480 | tf_op jit(solution)/shard_map/ppermute | solution.py:403
  47.6 16.3 %collective-permute-start.6 = (bf16[32,16,576]{2,1,0:T(8,128)(2,1)S(1)}, bf16[32,16,576]{2,1,0:T(8,128)(2,1)}, u32[]{:S(2)}, u32[]{:S(2)}) collective-permute-start(bf16[32,16,576]{2,1,0:T(8,128)(2,1)S(1)} %collective-permute-done.refs_0_), channel_id=1, source_target_pairs={{0,1},{1,0},{2,3},{3,2},{4,5},{5,4},{6,7},{7,6},{8,9},{9,8},{10,11... | collective-permute-start | bytes 1769480 | tf_op jit(solution)/shard_map/ppermute | solution.py:403
  47.6 16.3 %collective-permute-start.7 = (bf16[32,16,576]{2,1,0:T(8,128)(2,1)S(1)}, bf16[32,16,576]{2,1,0:T(8,128)(2,1)}, u32[]{:S(2)}, u32[]{:S(2)}) collective-permute-start(bf16[32,16,576]{2,1,0:T(8,128)(2,1)S(1)} %collective-permute-done.2.refs_1_), channel_id=1, source_target_pairs={{0,1},{1,0},{2,3},{3,2},{4,5},{5,4},{6,7},{7,6},{8,9},{9,8},{10,11... | collective-permute-start | bytes 1769480 | tf_op jit(solution)/shard_map/ppermute | solution.py:403
  48.4 15.0 %collective-permute-start.1 = (bf16[16,16,576]{2,1,0:T(8,128)(2,1)S(1)}, bf16[16,16,576]{2,1,0:T(8,128)(2,1)S(1)}, u32[]{:S(2)}, u32[]{:S(2)}) collective-permute-start(bf16[16,16,576]{2,1,0:T(8,128)(2,1)S(1)} %slice.50), channel_id=1, source_target_pairs={{0,2},{2,4},{4,6},{6,0},{1,3},{3,5},{5,7},{7,1},{8,10},{10,12},{12... | collective-permute-start | bytes 884744 | tf_op jit(solution)/shard_map/ppermute | solution.py:406
  49.2 14.2 %collective-permute-start.3 = (bf16[16,16,576]{2,1,0:T(8,128)(2,1)S(1)}, bf16[16,16,576]{2,1,0:T(8,128)(2,1)S(1)}, u32[]{:S(2)}, u32[]{:S(2)}) collective-permute-start(bf16[16,16,576]{2,1,0:T(8,128)(2,1)S(1)} %slice.51), channel_id=1, source_target_pairs={{0,6},{2,0},{4,2},{6,4},{1,7},{3,1},{5,3},{7,5},{8,14},{10,8},{12,... | collective-permute-start | bytes 884744 | tf_op jit(solution)/shard_map/ppermute | solution.py:406
  53.5 23.2 %slice-start = ((s8[14680064]{0:T(1024)(128)(4,1)}), s8[4194304]{0:T(1024)(128)(4,1)S(1)}, s32[]{:S(2)}) async-start(s8[14680064]{0:T(1024)(128)(4,1)} %bitcast.25), calls=%async_computation.1 | async-start | bytes 8388608
  53.5 23.2 %slice-start.1 = ((s8[14680064]{0:T(1024)(128)(4,1)}), s8[4194304]{0:T(1024)(128)(4,1)S(1)}, s32[]{:S(2)}) async-start(s8[14680064]{0:T(1024)(128)(4,1)} %bitcast.25), calls=%async_computation.2 | async-start | bytes 8388608
  63.4 13.4 %collective-permute-start.4 = (bf16[16,16,576]{2,1,0:T(8,128)(2,1)S(1)}, bf16[16,16,576]{2,1,0:T(8,128)(2,1)S(1)}, u32[]{:S(2)}, u32[]{:S(2)}) collective-permute-start(bf16[16,16,576]{2,1,0:T(8,128)(2,1)S(1)} %collective-permute-done.1.refs_0_), channel_id=1, source_target_pairs={{0,1},{1,0},{2,3},{3,2},{4,5},{5,4},{6,7},{7,6},{8,9},{9,8},{10,11... | collective-permute-start | bytes 884744 | tf_op jit(solution)/shard_map/ppermute | solution.py:403
  63.5 13.3 %collective-permute-start.5 = (bf16[16,16,576]{2,1,0:T(8,128)(2,1)S(1)}, bf16[16,16,576]{2,1,0:T(8,128)(2,1)S(1)}, u32[]{:S(2)}, u32[]{:S(2)}) collective-permute-start(bf16[16,16,576]{2,1,0:T(8,128)(2,1)S(1)} %collective-permute-done.3.refs_1_), channel_id=1, source_target_pairs={{0,1},{1,0},{2,3},{3,2},{4,5},{5,4},{6,7},{7,6},{8,9},{9,8},{10,11... | collective-permute-start | bytes 884744 | tf_op jit(solution)/shard_map/ppermute | solution.py:403
  64.0 12.8 %slice-start.2 = ((s8[14680064]{0:T(1024)(128)(4,1)}), s8[4194304]{0:T(1024)(128)(4,1)S(1)}, s32[]{:S(2)}) async-start(s8[14680064]{0:T(1024)(128)(4,1)} %bitcast.25), calls=%async_computation.3 | async-start | bytes 8388608
  64.0 12.8 %slice-start.3 = ((s8[14680064]{0:T(1024)(128)(4,1)}), s8[2097152]{0:T(1024)(128)(4,1)S(1)}, s32[]{:S(2)}) async-start(s8[14680064]{0:T(1024)(128)(4,1)} %bitcast.25), calls=%async_computation.4 | async-start | bytes 4194304
  85.7 5.8 %collective-permute-start.11 = (bf16[256,896]{1,0:T(8,128)(2,1)S(1)}, bf16[256,896]{1,0:T(8,128)(2,1)S(1)}, u32[]{:S(2)}, u32[]{:S(2)}) collective-permute-start(bf16[256,896]{1,0:T(8,128)(2,1)S(1)} %get-tuple-element.34), channel_id=1, source_target_pairs={{0,1},{1,0},{2,3},{3,2},{4,5},{5,4},{6,7},{7,6},{8,9},{9,8},{10,11... | collective-permute-start | bytes 1376264 | tf_op jit(solution)/shard_map/ppermute | solution.py:403
  89.0 6.0 %collective-permute-start.10 = (bf16[2,256,896]{2,1,0:T(8,128)(2,1)S(1)}, bf16[2,256,896]{2,1,0:T(8,128)(2,1)S(1)}, u32[]{:S(2)}, u32[]{:S(2)}) collective-permute-start(bf16[2,256,896]{2,1,0:T(8,128)(2,1)S(1)} %get-tuple-element.32), channel_id=1, source_target_pairs={{0,1},{1,0},{2,3},{3,2},{4,5},{5,4},{6,7},{7,6},{8,9},{9,8},{10,11... | collective-permute-start | bytes 2752520 | tf_op jit(solution)/shard_map/ppermute | solution.py:403
  91.2 13.8 %collective-permute-start.9 = (bf16[1,256,896]{2,1,0:T(8,128)(2,1)S(1)}, bf16[1,256,896]{2,1,0:T(8,128)(2,1)S(1)}, u32[]{:S(2)}, u32[]{:S(2)}) collective-permute-start(bf16[1,256,896]{2,1,0:T(8,128)(2,1)S(1)} %get-tuple-element.30), channel_id=1, source_target_pairs={{0,1},{1,0},{2,3},{3,2},{4,5},{5,4},{6,7},{7,6},{8,9},{9,8},{10,11... | collective-permute-start | bytes 1376264 | tf_op jit(solution)/shard_map/ppermute | solution.py:403
  91.7 9.8 %collective-permute-start.12 = (bf16[128,896]{1,0:T(8,128)(2,1)S(1)}, bf16[128,896]{1,0:T(8,128)(2,1)S(1)}, u32[]{:S(2)}, u32[]{:S(2)}) collective-permute-start(bf16[128,896]{1,0:T(8,128)(2,1)S(1)} %get-tuple-element.42), channel_id=1, source_target_pairs={{0,2},{2,4},{4,6},{6,0},{1,3},{3,5},{5,7},{7,1},{8,10},{10,12},{12... | collective-permute-start | bytes 688136 | tf_op jit(solution)/shard_map/ppermute | solution.py:406
  91.8 9.7 %collective-permute-start.16 = (bf16[128,896]{1,0:T(8,128)(2,1)S(1)}, bf16[128,896]{1,0:T(8,128)(2,1)S(1)}, u32[]{:S(2)}, u32[]{:S(2)}) collective-permute-start(bf16[128,896]{1,0:T(8,128)(2,1)S(1)} %get-tuple-element.41), channel_id=1, source_target_pairs={{0,6},{2,0},{4,2},{6,4},{1,7},{3,1},{5,3},{7,5},{8,14},{10,8},{12,... | collective-permute-start | bytes 688136 | tf_op jit(solution)/shard_map/ppermute | solution.py:406
  95.1 10.8 %collective-permute-start.14 = (bf16[128,896]{1,0:T(8,128)(2,1)S(1)}, bf16[128,896]{1,0:T(8,128)(2,1)S(1)}, u32[]{:S(2)}, u32[]{:S(2)}) collective-permute-start(bf16[128,896]{1,0:T(8,128)(2,1)S(1)} %get-tuple-element.40), channel_id=1, source_target_pairs={{0,6},{2,0},{4,2},{6,4},{1,7},{3,1},{5,3},{7,5},{8,14},{10,8},{12,... | collective-permute-start | bytes 688136 | tf_op jit(solution)/shard_map/ppermute | solution.py:406
  95.3 11.1 %collective-permute-start.15 = (bf16[128,896]{1,0:T(8,128)(2,1)S(1)}, bf16[128,896]{1,0:T(8,128)(2,1)S(1)}, u32[]{:S(2)}, u32[]{:S(2)}) collective-permute-start(bf16[128,896]{1,0:T(8,128)(2,1)S(1)} %get-tuple-element.39), channel_id=1, source_target_pairs={{0,2},{2,4},{4,6},{6,0},{1,3},{3,5},{5,7},{7,1},{8,10},{10,12},{12... | collective-permute-start | bytes 688136 | tf_op jit(solution)/shard_map/ppermute | solution.py:406
  101.6 8.9 %collective-permute-start.13 = (bf16[128,896]{1,0:T(8,128)(2,1)S(1)}, bf16[128,896]{1,0:T(8,128)(2,1)S(1)}, u32[]{:S(2)}, u32[]{:S(2)}) collective-permute-start(bf16[128,896]{1,0:T(8,128)(2,1)S(1)} %get-tuple-element.38), channel_id=1, source_target_pairs={{0,2},{2,4},{4,6},{6,0},{1,3},{3,5},{5,7},{7,1},{8,10},{10,12},{12... | collective-permute-start | bytes 688136 | tf_op jit(solution)/shard_map/ppermute | solution.py:406
  101.7 8.8 %collective-permute-start.17 = (bf16[128,896]{1,0:T(8,128)(2,1)S(1)}, bf16[128,896]{1,0:T(8,128)(2,1)S(1)}, u32[]{:S(2)}, u32[]{:S(2)}) collective-permute-start(bf16[128,896]{1,0:T(8,128)(2,1)S(1)} %get-tuple-element.37), channel_id=1, source_target_pairs={{0,6},{2,0},{4,2},{6,4},{1,7},{3,1},{5,3},{7,5},{8,14},{10,8},{12,... | collective-permute-start | bytes 688136 | tf_op jit(solution)/shard_map/ppermute | solution.py:406
  (9 other events, 50.0 us)

commit v2 on v1

--- a/solution.py
+++ b/solution.py
@@ -40,23 +40,57 @@
     return jnp.dot(a, b, preferred_element_type=jnp.float32)
 
 
+def send_kernel(index_ref, cache_ref, out_ref):
+    readers = out_ref.shape[0]
+    for r in range(readers):
+        for k in range(0, MOST, 2):
+            rotary = []
+            for i in range(2):
+                rows = cache_ref[index_ref[r, k + i]]
+                for b in range(4):
+                    out_ref[r, 4 * (k + i) + b] = rows[:, 128 * b : 128 * (b + 1)]
+                rotary.append(rows[:, 512:])
+            out_ref[r, 4 * MOST + k // 2] = jnp.concatenate(rotary, axis=1)
+
+
+def send(index, cache):
+    rows = cache.shape[1]
+    shape = (index.shape[0], 4 * MOST + MOST // 2, rows, 128)
+    return pl.pallas_call(
+        send_kernel,
+        name="send",
+        out_shape=jax.ShapeDtypeStruct(shape, cache.dtype),
+        in_specs=[sspec(), vspec()],
+        out_specs=vspec(),
+        compiler_params=params(4),
+    )(index, cache)
+
+
 def pick_kernel(slot_ref, list_ref, arrived_ref, cos_ref, sin_ref, out_ref):
-    latent = out_ref.shape[2] - 64
-    for j in range(out_ref.shape[0]):
-        rows = arrived_ref[slot_ref[j]]
-        out_ref[j, :, :latent] = rows[:, :latent]
-        rotary = rows[:, latent:].astype(jnp.float32)
-        swapped = jnp.concatenate([rotary[:, 32:], rotary[:, :32]], axis=1)
-        turned = rotary * cos_ref[j][None, :] + swapped * sin_ref[j][None, :]
-        out_ref[j, :, latent:] = turned.astype(jnp.bfloat16)
+    half = out_ref.shape[1] * 2 // 9
+    for j in range(0, 2 * half, 2):
+        h, i = j // half, j % half
+        pair = []
+        for e in range(2):
+            owner = slot_ref[j + e] >> 2
+            slot = slot_ref[j + e] & (MOST - 1)
+            for b in range(4):
+                out_ref[h, 4 * (i + e) + b] = arrived_ref[owner, 4 * slot + b]
+            both = arrived_ref[owner, 4 * MOST + (slot >> 1)].astype(jnp.float32)
+            rotary = jnp.where((slot & 1) == 1, both[:, 64:], both[:, :64])
+            swapped = jnp.concatenate([rotary[:, 32:], rotary[:, :32]], axis=1)
+            turned = rotary * cos_ref[j + e][None, :] + swapped * sin_ref[j + e][None, :]
+            pair.append(turned)
+        out_ref[h, 4 * half + i // 2] = jnp.concatenate(pair, axis=1).astype(jnp.bfloat16)
 
 
 def pick(slots, lists, arrived, cosines, sines):
-    count = slots.shape[0]
+    half = slots.shape[0] // 2
+    shape = (2, 4 * half + half // 2) + arrived.shape[2:]
     return pl.pallas_call(
         pick_kernel,
         name="pick",
-        out_shape=jax.ShapeDtypeStruct((count,) + arrived.shape[1:], jnp.bfloat16),
+        out_shape=jax.ShapeDtypeStruct(shape, jnp.bfloat16),
         in_specs=[sspec(), sspec(), vspec(), vspec(), vspec()],
         out_specs=vspec(),
         compiler_params=params(4),
@@ -66,7 +100,7 @@
 
 def start_kernel(place_ref, mask_ref, q_ref, uk_ref, q_out, list_out):
     heads, nope, latent = uk_ref.shape
-    rope = q_out.shape[2] - latent
+    rope = (q_out.shape[2] - latent) // 2
     width = nope + rope
     tiles = q_ref.shape[0] // TILE
     listed = mask_ref.shape[1]
@@ -86,7 +120,8 @@
         qr = q_ref[:, h * width + nope : (h + 1) * width]
         for t in range(tiles):
             q_out[t, h * TILE : (h + 1) * TILE, :latent] = ql[t * TILE : (t + 1) * TILE]
-            q_out[t, h * TILE : (h + 1) * TILE, latent:] = qr[t * TILE : (t + 1) * TILE]
+            twice = jnp.concatenate([qr[t * TILE : (t + 1) * TILE]] * 2, axis=1)
+            q_out[t, h * TILE : (h + 1) * TILE, latent:] = twice
 
 
 def start(place, tile_mask, queries, w_uk):
@@ -97,7 +132,7 @@
         start_kernel,
         name="start",
         out_shape=(
-            jax.ShapeDtypeStruct((tiles, heads * TILE, latent + rope), jnp.bfloat16),
+            jax.ShapeDtypeStruct((tiles, heads * TILE, latent + 2 * rope), jnp.bfloat16),
             jax.ShapeDtypeStruct((tiles, listed + 3), jnp.int32),
         ),
         in_specs=[sspec(), sspec(), vspec(), vspec()],
@@ -124,15 +159,30 @@
 
 
 def gather(halves, near):
-    spans = halves[0].shape[0]
     for i, half in enumerate(halves):
-        near[i // 2, (i % 2) * spans : (i % 2 + 1) * spans] = half[...]
-
-
-def attend(list_ref, q_ref, sources, scale, state, short):
+        near[i // 2, i % 2] = half[...]
+
+
+def sides(side_ref):
+    lane = lax.broadcasted_iota(jnp.int32, side_ref.shape[1:], 1)
+    for e in range(2):
+        side_ref[e] = jnp.where((lane >= 64) == (e == 1), 1.0, 0.0).astype(jnp.bfloat16)
+
+
+def span_rows(ref, j, side_ref):
+    half = ref.shape[1] * 2 // 9
+    h = (j >= half).astype(jnp.int32)
+    i = j - h * half
+    parts = [ref[h, 4 * i + b] for b in range(4)]
+    parts.append(ref[h, 4 * half + (i >> 1)] * side_ref[i & 1])
+    return jnp.concatenate(parts, axis=1)
+
+
+def attend(list_ref, q_ref, sources, scale, state, side_ref, short):
     latent = state[2].shape[2]
     tiles = q_ref.shape[0]
-    per = len(sources) * sources[0].shape[1]
+    sides(side_ref)
+    per = len(sources) * sources[0].shape[2]
     group = 512 // per
     room = list_ref.shape[1] - 3
     counts = [list_ref[t, room] for t in range(tiles)]
@@ -140,8 +190,9 @@
     def step(base, size, which):
         keys, scores = [], []
         for t in which:
+            spans = [list_ref[t, base + i] for i in range(size)]
             rows = jnp.concatenate(
-                [ref[list_ref[t, base + i]] for i in range(size) for ref in sources], axis=0
+                [span_rows(ref, j, side_ref) for j in spans for ref in sources], axis=0
             )
             s = dot_t(q_ref[t], rows)
             col = lax.broadcasted_iota(jnp.int32, s.shape, 1)
@@ -151,25 +202,28 @@
             fold(scores[i], keys[i][:, :latent], t, scale, state)
 
     low, high = jnp.minimum(counts[0], counts[1]), jnp.maximum(counts[0], counts[1])
-    longer = (counts[1] > counts[0]).astype(jnp.int32)
+    if not short:
+        low = high
     full = low // group
     left = low - full * group
     wide = left > group // 2 if short else left > 0
     steps = full + wide.astype(jnp.int32)
-    done = steps * group
 
     def body(g, carry):
         step(g * group, group, range(tiles))
         return carry
 
     lax.fori_loop(0, steps, body, 0)
-    if short:
-        narrow = jnp.logical_and(left > 0, left <= group // 2)
-        done = done + jnp.where(narrow, group // 2, 0)
-
-        @pl.when(narrow)
-        def _():
-            step(full * group, group // 2, range(tiles))
+    if not short:
+        return
+    narrow = jnp.logical_and(left > 0, left <= group // 2)
+    done = steps * group + jnp.where(narrow, group // 2, 0)
+
+    @pl.when(narrow)
+    def _():
+        step(full * group, group // 2, range(tiles))
+
+    longer = (counts[1] > counts[0]).astype(jnp.int32)
 
     def rest_of_longer(g, carry):
         step(done + g * group, group, (longer,))
@@ -179,12 +233,12 @@
 
 
 def first_kernel(list_ref, q_ref, own_ref, *refs, pieces, scale):
-    sources, state = refs[:pieces], refs[pieces:]
+    sources, state, side_ref = refs[:pieces], refs[pieces:-1], refs[-1]
     high_ref, sum_ref, acc_ref = state
     latent = acc_ref.shape[2]
     for t in range(q_ref.shape[0]):
         keys = own_ref[: (t + 1) * TILE]
-        s = dot_t(q_ref[t], keys)
+        s = dot_t(q_ref[t, :, : keys.shape[1]], keys)
         row = lax.broadcasted_iota(jnp.int32, s.shape, 0) % TILE + t * TILE
         col = lax.broadcasted_iota(jnp.int32, s.shape, 1)
         s = jnp.where(col <= row, s, NEG)
@@ -196,12 +250,15 @@
         high_ref[t] = jnp.broadcast_to(high, high_ref.shape[1:])
         sum_ref[t] = part
         acc_ref[t] = dot(p.astype(jnp.bfloat16), keys[:, :latent])
-    attend(list_ref, q_ref, sources, scale, state, False)
+    attend(list_ref, q_ref, sources, scale, state, side_ref, False)
 
 
 def near_scratch(halves):
-    shape = halves[0].shape
-    return pltpu.VMEM((len(halves) // 2, 2 * shape[0]) + shape[1:], halves[0].dtype)
+    return pltpu.VMEM((len(halves) // 2, 2) + halves[0].shape, halves[0].dtype)
+
+
+def side_scratch():
+    return pltpu.VMEM((2, 16, 128), jnp.bfloat16)
 
 
 def first(lists, q, own_rows, halves, latent, scale):
@@ -218,6 +275,7 @@
         ),
         in_specs=[sspec()] + [vspec()] * (len(args) - 1),
         out_specs=(vspec(),) * 3,
+        scratch_shapes=[side_scratch()],
         compiler_params=params(16),
         cost_estimate=cost(5e9, 2e7),
     )(*args)
@@ -225,10 +283,10 @@
 
 def stage_kernel(list_ref, q_ref, *refs, pieces, scale):
     sources = refs[:pieces]
-    source, state = refs[pieces : pieces + 3], refs[pieces + 3 : pieces + 6]
+    source, state, side_ref = refs[pieces : pieces + 3], refs[pieces + 3 : pieces + 6], refs[-1]
     for old, new in zip(source, state):
         new[...] = old[...]
-    attend(list_ref, q_ref, sources, scale, state, True)
+    attend(list_ref, q_ref, sources, scale, state, side_ref, True)
 
 
 def stage(lists, q, halves, state, scale):
@@ -240,6 +298,7 @@
         out_shape=tuple(jax.ShapeDtypeStruct(x.shape, x.dtype) for x in state),
         in_specs=[sspec()] + [vspec()] * (len(args) - 1),
         out_specs=(vspec(),) * 3,
+        scratch_shapes=[side_scratch()],
         input_output_aliases={before: 0, before + 1: 1, before + 2: 2},
         compiler_params=params(18),
         cost_estimate=cost(1e10, 2e7),
@@ -260,12 +319,12 @@
     uv_ref, wo_ref = refs[pieces : pieces + 2]
     source = refs[pieces + 2 : pieces + 5]
     out_ref, mine_ref, other_ref = refs[pieces + 5 : pieces + 8]
-    state, near = refs[pieces + 8 : pieces + 11], refs[pieces + 11]
+    state, near, side_ref = refs[pieces + 8 : pieces + 11], refs[-2], refs[-1]
     gather(halves, near)
     for old, new in zip(source, state):
         new[...] = old[...]
     sources = [near.at[i] for i in range(near.shape[0])]
-    attend(list_ref, q_ref, sources, scale, state, True)
+    attend(list_ref, q_ref, sources, scale, state, side_ref, True)
     for t in range(q_ref.shape[0]):
         total = jnp.sum(state[1][t], axis=1, keepdims=True)
         mixed = (state[2][t] / total).astype(jnp.bfloat16)
@@ -298,33 +357,34 @@
         in_specs=[sspec()] + [vspec()] * (len(args) - 1),
         out_specs=(vspec(),) * 6,
         input_output_aliases={before: 3, before + 1: 4, before + 2: 5},
-        scratch_shapes=[near_scratch(halves)],
+        scratch_shapes=[near_scratch(halves), side_scratch()],
         compiler_params=params(16),
         cost_estimate=cost(8e9, 2e7),
     )(*args)
     return outs[:3]
 
 
-def columns_kernel(list_ref, x_ref, wo_ref, other_ref, mine_ref, *, aways):
-    columns = other_ref.shape[2]
+def columns_kernel(list_ref, x_ref, wo_ref, *out_refs, parts):
     x = x_ref[...]
-    for i, away in enumerate(aways):
-        other_ref[i] = project(x, wo_ref, away, False, list_ref, columns)
-    for i, away in enumerate(aways):
-        mine_ref[i] = project(x, wo_ref, away, True, list_ref, columns)
-
-
-def columns_of(lists, head_out, w_o, aways):
+    for ref, (aways, mine) in zip(out_refs, parts):
+        for i, away in enumerate(aways):
+            ref[i] = project(x, wo_ref, away, mine, list_ref, ref.shape[2])
+
+
+def columns_of(lists, head_out, w_o, parts):
     tokens = head_out.shape[0]
-    shape = jax.ShapeDtypeStruct((len(aways), tokens, w_o.shape[1] // 8), jnp.bfloat16)
-    return pl.pallas_call(
-        functools.partial(columns_kernel, aways=aways),
+    columns = w_o.shape[1] // 8
+    count = sum(len(aways) for aways, _ in parts)
+    return pl.pallas_call(
+        functools.partial(columns_kernel, parts=parts),
         name="columns",
-        out_shape=(shape, shape),
+        out_shape=tuple(
+            jax.ShapeDtypeStruct((len(aways), tokens, columns), jnp.bfloat16) for aways, _ in parts
+        ),
         in_specs=[sspec(), vspec(), vspec()],
-        out_specs=(vspec(), vspec()),
+        out_specs=(vspec(),) * len(parts),
         compiler_params=params(8),
-        cost_estimate=cost(1e9 * len(aways), 4e6 * len(aways)),
+        cost_estimate=cost(5e8 * count, 2e6 * count),
     )(lists, head_out, w_o)
 
 
@@ -354,7 +414,6 @@
 
 def per_device(queries, own_latent, cache, block_list, offsets, tile_mask, w_uk, w_uv, w_o):
     seq = ("x", "y")
-    seq_count = lax.axis_size(seq)
     seq_index = lax.axis_index(seq)
     spans_held = cache.shape[0]
     listed_count = block_list.shape[1]
@@ -364,9 +423,12 @@
     width = w_uk.shape[1] + rope
     scale = width ** (-0.5)
 
-    owners = block_list // spans_held
-    within = block_list % spans_held
-    earlier = jnp.tril(jnp.ones((listed_count, listed_count), jnp.bool_), -1)
+    shift = spans_held.bit_length() - 1
+    assert spans_held == 1 << shift
+    owners = block_list >> shift
+    within = block_list & (spans_held - 1)
+    position = jnp.arange(listed_count, dtype=jnp.int32)
+    earlier = position[None, :] < position[:, None]
     same_owner = owners[:, :, None] == owners[:, None, :]
     ranking = jnp.sum(same_owner & earlier[None], axis=2)
     slot_ids = jnp.arange(MOST, dtype=jnp.int32)
@@ -375,7 +437,7 @@
     my_owners = lax.dynamic_index_in_dim(owners, seq_index, 0, keepdims=False)
     my_ranking = lax.dynamic_index_in_dim(ranking, seq_index, 0, keepdims=False)
     flat_slot = my_owners * MOST + my_ranking
-    sent = cache[send_index]
+    sent = send(send_index, cache)
     arrived = lax.all_to_all(sent, seq, split_axis=0, concat_axis=0, tiled=True)
 
     place = jnp.stack([lax.axis_index("z"), lax.axis_index("c")]).astype(jnp.int32)
@@ -390,7 +452,7 @@
     own = pick(
         flat_slot,
         lists,
-        arrived.reshape(seq_count * MOST, cache.shape[1], latent_full),
+        arrived,
         cosines,
         sines,
     )
@@ -409,9 +471,8 @@
     minus = move(own, down)
     twin = other_core(own)
     state = first(lists, q, own_latent, [own, twin], latent, scale)
-    half = own.shape[0] // 2
-    low = move(plus[:half], up)
-    high = move(minus[half:], down)
+    low = move(plus[0], up)
+    high = move(minus[1], down)
     pieces = [plus, minus]
     pieces = pieces + [other_core(x) for x in pieces]
     state = stage(lists, q, pieces, state, scale)
@@ -427,14 +488,17 @@
 
     h = far_mine.shape[0] // 2
     far_other = other_core(far_other)
-    others, mine = columns_of(lists, head_out, w_o, (1, 3))
+    (others,) = columns_of(lists, head_out, w_o, (((1, 3), False),))
     others = other_core(others)
     far = add(far_mine, far_other).astype(bf)
     below = move(far[:h], up)
     above = move(far[h:], down)
+    (mine,) = columns_of(lists, head_out, w_o, (((1, 3), True),))
     early_up = move(add(mine[0, h:], others[0, h:]).astype(bf), up)
     early_down = move(add(mine[1, :h], others[1, :h]).astype(bf), down)
-    kept_other, kept_mine = columns_of(lists, head_out, w_o, (0,))
+    kept_other, kept_mine = columns_of(
+        lists, head_out, w_o, (((0,), False), ((0,), True))
+    )
     late_up = move(add(mine[0, :h], others[0, :h], below).astype(bf), up)
     late_down = move(add(mine[1, h:], others[1, h:], above).astype(bf), down)
     kept_other = other_core(kept_other)

time: 112 us -> 110 us (0.982)
  the two profiles are of different devices: /device:TPU:8 before, /device:TPU:0 now
where the time goes in v2:
time: 110 us; the launch traced here: 108 us
  Pallas kernels  38.9 us (35%)
  waiting for transfers between devices  34.8 us (32%)
  starting transfers between devices  25.4 us (23%)
  local copies, waits for them, and re-layouts  5.84 us (5%)
  other arithmetic  2.74 us (2%)
    ppermute x10, waiting for transfers between devices, move(): return lax.ppermute(x, 'z', ways)  20.4 us
    ppermute x10, starting transfers between devices, move(): return lax.ppermute(x, 'z', ways)  16.3 us
    all_to_all x1, waiting for transfers between devices, per_device(): arrived = lax.all_to_all(sent, seq, split_axis=0, concat_axis=0, tiled=True)  14.4 us
    pallas_call x1, Pallas kernels, stage(): pl.pallas_call(functools.partial(stage_kernel, pieces=len(halves), scale=...  9.86 us
    pallas_call x1, Pallas kernels, first(): pl.pallas_call(functools.partial(first_kernel, pieces=len(halves), scale=...  9.09 us
    pallas_call x1, Pallas kernels, last(): pl.pallas_call(functools.partial(last_kernel, pieces=len(halves), scale=s...  8.61 us
    all_to_all x1, starting transfers between devices, per_device(): arrived = lax.all_to_all(sent, seq, split_axis=0, concat_axis=0, tiled=True)  7.15 us
    unnamed x27, local copies, waits for them, and re-layouts  5.67 us
  transfers between devices with their start and end apart: 19, of which 6 were waited for; matrix products, arithmetic and copies ran while one was open for 1% of the time, Pallas kernels for 24%

profile of v2, /device:TPU:0, one launch (start us, length us, event | category | flops | bytes accessed | tf_op | source)
XLA Modules:
  0.0 108.0 jit_solution(1899484942919026285)
XLA Ops:
  2.1 1.1 %copy-done = bf16[32,16,576]{2,1,0:T(8,128)(2,1)S(1)} copy-done((bf16[32,16,576]{2,1,0:T(8,128)(2,1)S(1)}, bf16[32,16,576]{2,1,0:T(8,128)(2,1)}, u32[]{:S(2)}) %copy-start) | copy-done | bytes 589848
  3.2 1.9 %send.1 = bf16[16,18,16,128]{3,2,1,0:T(8,128)(2,1)} custom-call(s32[16,4]{1,0:T(8,128)S(1)} %copy.17.index_ref, bf16[32,16,576]{2,1,0:T(8,128)(2,1)S(1)} %copy-done), custom_call_target="tpu_custom_call" | custom-call | tf_op jit(solution)/shard_map/send/pallas_call | solution.py:59
  5.1 7.1 %all-to-all-start = ((bf16[16,18,16,128]{3,2,1,0:T(8,128)(2,1)}), bf16[16,18,16,128]{3,2,1,0:T(8,128)(2,1)S(1)}, u32[]{:S(2)}, u32[]{:S(2)}) async-start(bf16[16,18,16,128]{3,2,1,0:T(8,128)(2,1)} %send.1), calls=%async_computation | async-start | bytes 2359296 | tf_op jit(solution)/shard_map/all_to_all | solution.py:441
  12.7 1.1 %copy-done.3 = bf16[256,1536]{1,0:T(8,128)(2,1)S(1)} copy-done((bf16[256,1536]{1,0:T(8,128)(2,1)S(1)}, bf16[256,1536]{1,0:T(8,128)(2,1)}, u32[]{:S(2)}) %copy-start.3) | copy-done | bytes 786456
  13.8 1.9 %start.1 = (bf16[2,1024,640]{2,1,0:T(8,128)(2,1)S(1)}, s32[2,35]{1,0:T(2,128)S(1)}) custom-call(s32[2]{0:T(128)S(1)} %pad_add_fusion.place_ref, s32[2,32]{1,0:T(2,128)S(1)} %bitcast.25, bf16[256,1536]{1,0:T(8,128)(2,1)S(1)} %copy-done.3, bf16[8,128,512]{2,1,0:T(8,128)(2,1)S(1)} %copy-done.1), custom_call_target="tpu_custom_call" | custom-call | flops 4000000000 | bytes 8000000 | tf_op jit(solution)/shard_map/start/pallas_call | solution.py:131
  15.7 1.5 %copy-done.5 = bf16[2,1024,640]{2,1,0:T(8,128)(2,1)} copy-done((bf16[2,1024,640]{2,1,0:T(8,128)(2,1)}, bf16[2,1024,640]{2,1,0:T(8,128)(2,1)S(1)}, u32[]{:S(2)}) %copy-start.5) | copy-done | bytes 2621464
  17.2 14.4 %all-to-all-done.arrived_ref = bf16[16,18,16,128]{3,2,1,0:T(8,128)(2,1)S(1)} async-done(((bf16[16,18,16,128]{3,2,1,0:T(8,128)(2,1)}), bf16[16,18,16,128]{3,2,1,0:T(8,128)(2,1)S(1)}, u32[]{:S(2)}, u32[]{:S(2)}) %all-to-all-start) | async-done | bytes 1179680 | tf_op jit(solution)/shard_map/all_to_all | solution.py:441
  31.6 1.1 pick.1.refs_0_
  32.6 2.0 %collective-permute-start = (bf16[2,72,16,128]{3,2,1,0:T(8,128)(2,1)S(1)}, bf16[2,72,16,128]{3,2,1,0:T(8,128)(2,1)S(1)}, u32[]{:S(2)}, u32[]{:S(2)}) collective-permute-start(bf16[2,72,16,128]{3,2,1,0:T(8,128)(2,1)S(1)} %pick.1.refs_0_), channel_id=1, source_target_pairs={{0,2},{2,4},{4,6},{6,0},{1,3},{3,5},{5,7},{7,1},{8,10},{10,12},{12... | collective-permute-start | bytes 1769480 | tf_op jit(solution)/shard_map/ppermute | solution.py:468
  34.6 2.2 %collective-permute-start.2 = (bf16[2,72,16,128]{3,2,1,0:T(8,128)(2,1)S(1)}, bf16[2,72,16,128]{3,2,1,0:T(8,128)(2,1)S(1)}, u32[]{:S(2)}, u32[]{:S(2)}) collective-permute-start(bf16[2,72,16,128]{3,2,1,0:T(8,128)(2,1)S(1)} %pick.1.refs_0_), channel_id=1, source_target_pairs={{0,6},{2,0},{4,2},{6,4},{1,7},{3,1},{5,3},{7,5},{8,14},{10,8},{12,... | collective-permute-start | bytes 1769480 | tf_op jit(solution)/shard_map/ppermute | solution.py:468
  37.0 10.5 %collective-permute-done.refs_0_ = bf16[2,72,16,128]{3,2,1,0:T(8,128)(2,1)S(1)} collective-permute-done((bf16[2,72,16,128]{3,2,1,0:T(8,128)(2,1)S(1)}, bf16[2,72,16,128]{3,2,1,0:T(8,128)(2,1)S(1)}, u32[]{:S(2)}, u32[]{:S(2)}) %collective-permute-start) | collective-permute-done | bytes 589856 | tf_op jit(solution)/shard_map/ppermute | solution.py:468
  48.2 3.2 %collective-permute-start.3 = (bf16[72,16,128]{2,1,0:T(8,128)(2,1)S(1)}, bf16[72,16,128]{2,1,0:T(8,128)(2,1)S(1)}, u32[]{:S(2)}, u32[]{:S(2)}) collective-permute-start(bf16[72,16,128]{2,1,0:T(8,128)(2,1)S(1)} %slice_bitcast_fusion), channel_id=1, source_target_pairs={{0,6},{2,0},{4,2},{6,4},{1,7},{3,1},{5,3},{7,5},{8,14},{10,8},{12,... | collective-permute-start | bytes 884744 | tf_op jit(solution)/shard_map/ppermute | solution.py:468
  51.4 1.7 %copy-done.6 = bf16[2,1024,640]{2,1,0:T(8,128)(2,1)S(1)} copy-done((bf16[2,1024,640]{2,1,0:T(8,128)(2,1)S(1)}, bf16[2,1024,640]{2,1,0:T(8,128)(2,1)}, u32[]{:S(2)}) %copy-start.6) | copy-done | bytes 2621464
  53.2 9.1 %first.1 = (f32[2,1024,128]{2,1,0:T(8,128)S(1)}, f32[2,1024,128]{2,1,0:T(8,128)S(1)}, f32[2,1024,512]{2,1,0:T(8,128)S(1)}) custom-call(s32[2,35]{1,0:T(2,128)S(1)} %get-tuple-element.18.list_ref, bf16[2,1024,640]{2,1,0:T(8,128)(2,1)S(1)} %copy-done.6, bf16[256,576]{1,0:T(8,128)(2,1)S(1)} %copy.18.own_ref, bf16[2,72,16,128]{3,2,1,0:T(8,128)(2,1)S(1)} %pick.1.refs_0_, ...), custom_call_target="tpu_custom_call" | custom-call | flops 5000000000 | bytes 20000000 | tf_op jit(solution)/shard_map/first/pallas_call | solution.py:268
  62.9 9.9 %stage.1 = (f32[2,1024,128]{2,1,0:T(8,128)S(1)}, f32[2,1024,128]{2,1,0:T(8,128)S(1)}, f32[2,1024,512]{2,1,0:T(8,128)S(1)}) custom-call(s32[2,35]{1,0:T(2,128)S(1)} %get-tuple-element.18.list_ref, bf16[2,1024,640]{2,1,0:T(8,128)(2,1)S(1)} %copy-done.6, ...), custom_call_target="tpu_custom_call", output_to_operand_aliasing={{0}: (6, {}), {1}: (7, {}), {2}: (8, {})} | custom-call | flops 10000000000 | bytes 20000000 | tf_op jit(solution)/shard_map/stage/pallas_call | solution.py:295
  72.9 8.6 %last.1 = (bf16[256,1024]{1,0:T(8,128)(2,1)S(1)}, bf16[256,896]{1,0:T(8,128)(2,1)S(1)}, bf16[256,896]{1,0:T(8,128)(2,1)S(1)}, f32[2,1024,128]{2,1,0:T(8,128)S(1)...) custom-call(s32[2,35]{1,0:T(2,128)S(1)} %get-tuple-element.18.list_r, ...), custom_call_target="tpu_custom_call", output_to_operand_aliasing={{3}: (8, {}), {4}: (9, {}), {5}: (10, {})} | custom-call | flops 8000000000 | bytes 20000000 | tf_op jit(solution)/shard_map/last/pallas_call | solution.py:348
  81.6 1.8 %columns.5 = bf16[2,256,896]{2,1,0:T(8,128)(2,1)S(1)} custom-call(s32[2,35]{1,0:T(2,128)S(1)} %get-tuple-element.18.list_ref, bf16[256,1024]{1,0:T(8,128)(2,1)S(1)} %get-tuple-element.26.x_ref, bf16[1024,7168]{1,0:T(8,128)(2,1)S(1)} %bitcast.24), custom_call_target="tpu_custom_call" | custom-call | flops 1000000000 | bytes 4000000 | tf_op jit(solution)/shard_map/columns/pallas_call | solution.py:378
  84.0 1.8 %columns.3 = (bf16[1,256,896]{2,1,0:T(8,128)(2,1)S(1)}, bf16[1,256,896]{2,1,0:T(8,128)(2,1)S(1)}) custom-call(s32[2,35]{1,0:T(2,128)S(1)} %get-tuple-element.18.list_ref, bf16[256,1024]{1,0:T(8,128)(2,1)S(1)} %get-tuple-element.26.x_ref, bf16[1024,7168]{1,0:T(8,128)(2,1)S(1)} %bitcast.24), custom_call_target="tpu_custom_call" | custom-call | flops 1000000000 | bytes 4000000 | tf_op jit(solution)/shard_map/columns/pallas_call | solution.py:378
  86.0 1.8 %columns.4 = bf16[2,256,896]{2,1,0:T(8,128)(2,1)S(1)} custom-call(s32[2,35]{1,0:T(2,128)S(1)} %get-tuple-element.18.list_ref, bf16[256,1024]{1,0:T(8,128)(2,1)S(1)} %get-tuple-element.26.x_ref, bf16[1024,7168]{1,0:T(8,128)(2,1)S(1)} %bitcast.24), custom_call_target="tpu_custom_call" | custom-call | flops 1000000000 | bytes 4000000 | tf_op jit(solution)/shard_map/columns/pallas_call | solution.py:378
  88.1 3.2 %collective-permute-start.16 = (bf16[128,896]{1,0:T(8,128)(2,1)S(1)}, bf16[128,896]{1,0:T(8,128)(2,1)S(1)}, u32[]{:S(2)}, u32[]{:S(2)}) collective-permute-start(bf16[128,896]{1,0:T(8,128)(2,1)S(1)} %get-tuple-element.35), channel_id=1, source_target_pairs={{0,6},{2,0},{4,2},{6,4},{1,7},{3,1},{5,3},{7,5},{8,14},{10,8},{12,... | collective-permute-start | bytes 688136 | tf_op jit(solution)/shard_map/ppermute | solution.py:468
  91.7 1.8 %collective-permute-start.15 = (bf16[128,896]{1,0:T(8,128)(2,1)S(1)}, bf16[128,896]{1,0:T(8,128)(2,1)S(1)}, u32[]{:S(2)}, u32[]{:S(2)}) collective-permute-start(bf16[128,896]{1,0:T(8,128)(2,1)S(1)} %get-tuple-element.33), channel_id=1, source_target_pairs={{0,2},{2,4},{4,6},{6,0},{1,3},{3,5},{5,7},{7,1},{8,10},{10,12},{12... | collective-permute-start | bytes 688136 | tf_op jit(solution)/shard_map/ppermute | solution.py:468
  93.5 4.2 %collective-permute-done.12 = bf16[128,896]{1,0:T(8,128)(2,1)S(1)} collective-permute-done((bf16[128,896]{1,0:T(8,128)(2,1)S(1)}, bf16[128,896]{1,0:T(8,128)(2,1)S(1)}, u32[]{:S(2)}, u32[]{:S(2)}) %collective-permute-start.12) | collective-permute-done | bytes 229408 | tf_op jit(solution)/shard_map/ppermute | solution.py:468
  98.0 3.3 %collective-permute-start.17 = (bf16[128,896]{1,0:T(8,128)(2,1)S(1)}, bf16[128,896]{1,0:T(8,128)(2,1)S(1)}, u32[]{:S(2)}, u32[]{:S(2)}) collective-permute-start(bf16[128,896]{1,0:T(8,128)(2,1)S(1)} %get-tuple-element.31), channel_id=1, source_target_pairs={{0,6},{2,0},{4,2},{6,4},{1,7},{3,1},{5,3},{7,5},{8,14},{10,8},{12,... | collective-permute-start | bytes 688136 | tf_op jit(solution)/shard_map/ppermute | solution.py:468
  102.7 4.4 %collective-permute-done.13.refs_0_ = bf16[128,896]{1,0:T(8,128)(2,1)S(1)} collective-permute-done((bf16[128,896]{1,0:T(8,128)(2,1)S(1)}, bf16[128,896]{1,0:T(8,128)(2,1)S(1)}, u32[]{:S(2)}, u32[]{:S(2)}) %collective-permute-start.13) | collective-permute-done | bytes 229408 | tf_op jit(solution)/shard_map/ppermute | solution.py:468
  (70 shorter events, 8.1 us)
Async XLA Ops:
  0.0 12.4 %copy-start.8 = (s32[1,32]{1,0:T(1,128)S(1)}, s32[1,32]{1,0:T(1,128)}, u32[]{:S(2)}) copy-start(s32[1,32]{1,0:T(1,128)} %param.13) | copy-start | bytes 388
  0.0 12.6 %copy-start.4 = (s32[1,2,32]{2,1,0:T(2,128)S(1)}, s32[1,2,32]{2,1,0:T(2,128)}, u32[]{:S(2)}) copy-start(s32[1,2,32]{2,1,0:T(2,128)} %param.14) | copy-start | bytes 772
  5.1 26.5 %all-to-all-start = ((bf16[16,18,16,128]{3,2,1,0:T(8,128)(2,1)}), bf16[16,18,16,128]{3,2,1,0:T(8,128)(2,1)S(1)}, u32[]{:S(2)}, u32[]{:S(2)}) async-start(bf16[16,18,16,128]{3,2,1,0:T(8,128)(2,1)} %send.1), calls=%async_computation | async-start | bytes 2359296 | tf_op jit(solution)/shard_map/all_to_all | solution.py:441
  13.8 23.1 %copy-start.7 = (bf16[256,576]{0,1:T(8,128)(2,1)S(1)}, bf16[256,576]{0,1:T(8,128)(2,1)}, u32[]{:S(2)}) copy-start(bf16[256,576]{0,1:T(8,128)(2,1)} %param.10) | copy-start | bytes 884740
  32.6 14.9 %collective-permute-start = (bf16[2,72,16,128]{3,2,1,0:T(8,128)(2,1)S(1)}, bf16[2,72,16,128]{3,2,1,0:T(8,128)(2,1)S(1)}, u32[]{:S(2)}, u32[]{:S(2)}) collective-permute-start(bf16[2,72,16,128]{3,2,1,0:T(8,128)(2,1)S(1)} %pick.1.refs_0_), channel_id=1, source_target_pairs={{0,2},{2,4},{4,6},{6,0},{1,3},{3,5},{5,7},{7,1},{8,10},{10,12},{12... | collective-permute-start | bytes 1769480 | tf_op jit(solution)/shard_map/ppermute | solution.py:468
  34.6 13.1 %collective-permute-start.2 = (bf16[2,72,16,128]{3,2,1,0:T(8,128)(2,1)S(1)}, bf16[2,72,16,128]{3,2,1,0:T(8,128)(2,1)S(1)}, u32[]{:S(2)}, u32[]{:S(2)}) collective-permute-start(bf16[2,72,16,128]{3,2,1,0:T(8,128)(2,1)S(1)} %pick.1.refs_0_), channel_id=1, source_target_pairs={{0,6},{2,0},{4,2},{6,4},{1,7},{3,1},{5,3},{7,5},{8,14},{10,8},{12,... | collective-permute-start | bytes 1769480 | tf_op jit(solution)/shard_map/ppermute | solution.py:468
  36.8 14.6 %collective-permute-start.8 = (bf16[2,72,16,128]{3,2,1,0:T(8,128)(2,1)S(1)}, bf16[2,72,16,128]{3,2,1,0:T(8,128)(2,1)S(1)}, u32[]{:S(2)}, u32[]{:S(2)}) collective-permute-start(bf16[2,72,16,128]{3,2,1,0:T(8,128)(2,1)S(1)} %pick.1.refs_0_), channel_id=1, source_target_pairs={{0,1},{1,0},{2,3},{3,2},{4,5},{5,4},{6,7},{7,6},{8,9},{9,8},{10,11... | collective-permute-start | bytes 1769480 | tf_op jit(solution)/shard_map/ppermute | solution.py:465
  47.5 14.8 %collective-permute-start.1 = (bf16[72,16,128]{2,1,0:T(8,128)(2,1)S(1)}, bf16[72,16,128]{2,1,0:T(8,128)(2,1)S(1)}, u32[]{:S(2)}, u32[]{:S(2)}) collective-permute-start(bf16[72,16,128]{2,1,0:T(8,128)(2,1)S(1)} %slice_bitcast_fusion.1), channel_id=1, source_target_pairs={{0,2},{2,4},{4,6},{6,0},{1,3},{3,5},{5,7},{7,1},{8,10},{10,12},{12... | collective-permute-start | bytes 884744 | tf_op jit(solution)/shard_map/ppermute | solution.py:468
  47.6 15.3 %collective-permute-start.6 = (bf16[2,72,16,128]{3,2,1,0:T(8,128)(2,1)S(1)}, bf16[2,72,16,128]{3,2,1,0:T(8,128)(2,1)S(1)}, u32[]{:S(2)}, u32[]{:S(2)}) collective-permute-start(bf16[2,72,16,128]{3,2,1,0:T(8,128)(2,1)S(1)} %collective-permute-done.refs_0_), channel_id=1, source_target_pairs={{0,1},{1,0},{2,3},{3,2},{4,5},{5,4},{6,7},{7,6},{8,9},{9,8},{10,11... | collective-permute-start | bytes 1769480 | tf_op jit(solution)/shard_map/ppermute | solution.py:465
  47.7 15.2 %collective-permute-start.7 = (bf16[2,72,16,128]{3,2,1,0:T(8,128)(2,1)S(1)}, bf16[2,72,16,128]{3,2,1,0:T(8,128)(2,1)S(1)}, u32[]{:S(2)}, u32[]{:S(2)}) collective-permute-start(bf16[2,72,16,128]{3,2,1,0:T(8,128)(2,1)S(1)} %collective-permute-done.2.refs_1_), channel_id=1, source_target_pairs={{0,1},{1,0},{2,3},{3,2},{4,5},{5,4},{6,7},{7,6},{8,9},{9,8},{10,11... | collective-permute-start | bytes 1769480 | tf_op jit(solution)/shard_map/ppermute | solution.py:465
  48.2 14.2 %collective-permute-start.3 = (bf16[72,16,128]{2,1,0:T(8,128)(2,1)S(1)}, bf16[72,16,128]{2,1,0:T(8,128)(2,1)S(1)}, u32[]{:S(2)}, u32[]{:S(2)}) collective-permute-start(bf16[72,16,128]{2,1,0:T(8,128)(2,1)S(1)} %slice_bitcast_fusion), channel_id=1, source_target_pairs={{0,6},{2,0},{4,2},{6,4},{1,7},{3,1},{5,3},{7,5},{8,14},{10,8},{12,... | collective-permute-start | bytes 884744 | tf_op jit(solution)/shard_map/ppermute | solution.py:468
  53.2 19.6 %slice-start = ((s8[14680064]{0:T(1024)(128)(4,1)}), s8[4194304]{0:T(1024)(128)(4,1)S(1)}, s32[]{:S(2)}) async-start(s8[14680064]{0:T(1024)(128)(4,1)} %bitcast.23), calls=%async_computation.1 | async-start | bytes 8388608
  53.2 19.6 %slice-start.1 = ((s8[14680064]{0:T(1024)(128)(4,1)}), s8[4194304]{0:T(1024)(128)(4,1)S(1)}, s32[]{:S(2)}) async-start(s8[14680064]{0:T(1024)(128)(4,1)} %bitcast.23), calls=%async_computation.2 | async-start | bytes 8388608
  62.3 10.5 %collective-permute-start.4 = (bf16[72,16,128]{2,1,0:T(8,128)(2,1)S(1)}, bf16[72,16,128]{2,1,0:T(8,128)(2,1)S(1)}, u32[]{:S(2)}, u32[]{:S(2)}) collective-permute-start(bf16[72,16,128]{2,1,0:T(8,128)(2,1)S(1)} %collective-permute-done.1.refs_0_), channel_id=1, source_target_pairs={{0,1},{1,0},{2,3},{3,2},{4,5},{5,4},{6,7},{7,6},{8,9},{9,8},{10,11... | collective-permute-start | bytes 884744 | tf_op jit(solution)/shard_map/ppermute | solution.py:465
  62.4 10.4 %collective-permute-start.5 = (bf16[72,16,128]{2,1,0:T(8,128)(2,1)S(1)}, bf16[72,16,128]{2,1,0:T(8,128)(2,1)S(1)}, u32[]{:S(2)}, u32[]{:S(2)}) collective-permute-start(bf16[72,16,128]{2,1,0:T(8,128)(2,1)S(1)} %collective-permute-done.3.refs_1_), channel_id=1, source_target_pairs={{0,1},{1,0},{2,3},{3,2},{4,5},{5,4},{6,7},{7,6},{8,9},{9,8},{10,11... | collective-permute-start | bytes 884744 | tf_op jit(solution)/shard_map/ppermute | solution.py:465
  81.5 6.3 %collective-permute-start.11 = (bf16[256,896]{1,0:T(8,128)(2,1)S(1)}, bf16[256,896]{1,0:T(8,128)(2,1)S(1)}, u32[]{:S(2)}, u32[]{:S(2)}) collective-permute-start(bf16[256,896]{1,0:T(8,128)(2,1)S(1)} %get-tuple-element.30), channel_id=1, source_target_pairs={{0,1},{1,0},{2,3},{3,2},{4,5},{5,4},{6,7},{7,6},{8,9},{9,8},{10,11... | collective-permute-start | bytes 1376264 | tf_op jit(solution)/shard_map/ppermute | solution.py:465
  83.5 7.8 %collective-permute-start.10 = (bf16[2,256,896]{2,1,0:T(8,128)(2,1)S(1)}, bf16[2,256,896]{2,1,0:T(8,128)(2,1)S(1)}, u32[]{:S(2)}, u32[]{:S(2)}) collective-permute-start(bf16[2,256,896]{2,1,0:T(8,128)(2,1)S(1)} %columns.5), channel_id=1, source_target_pairs={{0,1},{1,0},{2,3},{3,2},{4,5},{5,4},{6,7},{7,6},{8,9},{9,8},{10,11... | collective-permute-start | bytes 2752520 | tf_op jit(solution)/shard_map/ppermute | solution.py:465
  85.8 15.5 %collective-permute-start.9 = (bf16[1,256,896]{2,1,0:T(8,128)(2,1)S(1)}, bf16[1,256,896]{2,1,0:T(8,128)(2,1)S(1)}, u32[]{:S(2)}, u32[]{:S(2)}) collective-permute-start(bf16[1,256,896]{2,1,0:T(8,128)(2,1)S(1)} %get-tuple-element.28), channel_id=1, source_target_pairs={{0,1},{1,0},{2,3},{3,2},{4,5},{5,4},{6,7},{7,6},{8,9},{9,8},{10,11... | collective-permute-start | bytes 1376264 | tf_op jit(solution)/shard_map/ppermute | solution.py:465
  88.0 9.8 %collective-permute-start.12 = (bf16[128,896]{1,0:T(8,128)(2,1)S(1)}, bf16[128,896]{1,0:T(8,128)(2,1)S(1)}, u32[]{:S(2)}, u32[]{:S(2)}) collective-permute-start(bf16[128,896]{1,0:T(8,128)(2,1)S(1)} %get-tuple-element.36), channel_id=1, source_target_pairs={{0,2},{2,4},{4,6},{6,0},{1,3},{3,5},{5,7},{7,1},{8,10},{10,12},{12... | collective-permute-start | bytes 688136 | tf_op jit(solution)/shard_map/ppermute | solution.py:468
  88.1 9.7 %collective-permute-start.16 = (bf16[128,896]{1,0:T(8,128)(2,1)S(1)}, bf16[128,896]{1,0:T(8,128)(2,1)S(1)}, u32[]{:S(2)}, u32[]{:S(2)}) collective-permute-start(bf16[128,896]{1,0:T(8,128)(2,1)S(1)} %get-tuple-element.35), channel_id=1, source_target_pairs={{0,6},{2,0},{4,2},{6,4},{1,7},{3,1},{5,3},{7,5},{8,14},{10,8},{12,... | collective-permute-start | bytes 688136 | tf_op jit(solution)/shard_map/ppermute | solution.py:468
  91.4 10.8 %collective-permute-start.14 = (bf16[128,896]{1,0:T(8,128)(2,1)S(1)}, bf16[128,896]{1,0:T(8,128)(2,1)S(1)}, u32[]{:S(2)}, u32[]{:S(2)}) collective-permute-start(bf16[128,896]{1,0:T(8,128)(2,1)S(1)} %get-tuple-element.34), channel_id=1, source_target_pairs={{0,6},{2,0},{4,2},{6,4},{1,7},{3,1},{5,3},{7,5},{8,14},{10,8},{12,... | collective-permute-start | bytes 688136 | tf_op jit(solution)/shard_map/ppermute | solution.py:468
  91.7 10.9 %collective-permute-start.15 = (bf16[128,896]{1,0:T(8,128)(2,1)S(1)}, bf16[128,896]{1,0:T(8,128)(2,1)S(1)}, u32[]{:S(2)}, u32[]{:S(2)}) collective-permute-start(bf16[128,896]{1,0:T(8,128)(2,1)S(1)} %get-tuple-element.33), channel_id=1, source_target_pairs={{0,2},{2,4},{4,6},{6,0},{1,3},{3,5},{5,7},{7,1},{8,10},{10,12},{12... | collective-permute-start | bytes 688136 | tf_op jit(solution)/shard_map/ppermute | solution.py:468
  97.9 9.1 %collective-permute-start.13 = (bf16[128,896]{1,0:T(8,128)(2,1)S(1)}, bf16[128,896]{1,0:T(8,128)(2,1)S(1)}, u32[]{:S(2)}, u32[]{:S(2)}) collective-permute-start(bf16[128,896]{1,0:T(8,128)(2,1)S(1)} %get-tuple-element.32), channel_id=1, source_target_pairs={{0,2},{2,4},{4,6},{6,0},{1,3},{3,5},{5,7},{7,1},{8,10},{10,12},{12... | collective-permute-start | bytes 688136 | tf_op jit(solution)/shard_map/ppermute | solution.py:468
  98.0 9.0 %collective-permute-start.17 = (bf16[128,896]{1,0:T(8,128)(2,1)S(1)}, bf16[128,896]{1,0:T(8,128)(2,1)S(1)}, u32[]{:S(2)}, u32[]{:S(2)}) collective-permute-start(bf16[128,896]{1,0:T(8,128)(2,1)S(1)} %get-tuple-element.31), channel_id=1, source_target_pairs={{0,6},{2,0},{4,2},{6,4},{1,7},{3,1},{5,3},{7,5},{8,14},{10,8},{12,... | collective-permute-start | bytes 688136 | tf_op jit(solution)/shard_map/ppermute | solution.py:468
  (8 other events, 44.7 us)
